TPU v7x, 32 devices: a whole 2x2x4 slice. The times are simulated.
32 devices in a mesh: grp: 16 (over z, y, x), box: 2 (over core).
Axes of the slice: x: 2, y: 2, z: 4, core: 2. Of those that a mesh axis runs over, the one named last changes fastest.
Arguments:
- fine_state: float32 [16, 5, 8, 16, 256], P('grp', None, 'box'), may hold values from -1 to 6, as said below
- patch_ghosts: float32 [16, 2, 2, 5, 16, 256], P('grp'), may hold values from -1 to 6, as said below
- coarse_state: float32 [16, 2, 24, 5, 128], P('grp', 'box'), may hold values from -1 to 6, as said below
- coarse_face_term: float32 [16, 2, 24, 5, 128], P('grp', 'box'), may hold values from -1 to 1
- dest_grp: int32 [16, 2, 24], P('grp', 'box'), may hold values from 0 to 15, as said below
- dest_column: int32 [16, 2, 24], P('grp', 'box'), may hold values from 0 to 23, as said below
Outputs:
- fine_new: float32 [16, 5, 8, 16, 256], P('grp', None, 'box')
- coarse_new: float32 [16, 2, 24, 5, 128], P('grp', 'box')
Inputs may be any that keep to these rules, and one draw needn't show every extreme that they name: `fine_state`: every cell has density in 1 to 2, velocity components in -0.5 to 0.5 and pressure in 1 to 2. `patch_ghosts`: every cell has density in 1 to 2, velocity components in -0.5 to 0.5 and pressure in 1 to 2. `coarse_state`: every cell has density in 1 to 2, velocity components in -0.5 to 0.5 and pressure in 1 to 2. `dest_grp`: for each box index, each owner's columns receive exactly one record each; one box sends at most 2 and at least 1 records to each owner. `dest_column`: see dest_grp.
All inputs are finite; a program needn't handle non-finite values.
Results may differ from a plain program's by a relative error of at most 0.0001.
Values sent between devices are 32-bit elements; how exact they have to be, the bound alone decides.
No kernel may reach another device: no remote copies, remote signals or barrier semaphores. Data moves between devices by JAX's collectives and lax.ppermute only.
A program may use at most 64 MiB of HBM per device.

v0:
```python
import jax
import jax.numpy as jnp
from jax import lax
from jax.sharding import PartitionSpec as P

gamma_ratio = 1.4
time_step = 0.06


def extended_2(cells, sides, width):
    for axis, dim in sides:
        count = lax.axis_size(axis)
        ends = count - 1
        head = lax.slice_in_dim(cells, 0, width, axis=dim)
        tail = lax.slice_in_dim(cells, cells.shape[dim] - width, cells.shape[dim], axis=dim)
        cells = jnp.concatenate(
            [
                lax.ppermute(tail, axis, [(i, (i + 1) % count) for i in range(ends)]),
                cells,
                lax.ppermute(head, axis, [((i + 1) % count, i) for i in range(ends)]),
            ],
            axis=dim,
        )
    return cells


def cell_values(conserved):
    density = conserved[0]
    velocity = conserved[1:4] / density
    kinetic = 0.5 * jnp.sum(conserved[1:4] * velocity, axis=0)
    pressure = (gamma_ratio - 1.0) * (conserved[4] - kinetic)
    sound_speed = jnp.sqrt(gamma_ratio * pressure / density)
    return (velocity, pressure, sound_speed)


def physical_flux(conserved, velocity, pressure, normal):
    moving = velocity[normal]
    pieces = [conserved[1 + normal]]
    for member in range(3):
        if member == normal:
            pieces.append(conserved[1 + member] * moving + pressure)
        else:
            pieces.append(conserved[1 + member] * moving)
    pieces.append((conserved[4] + pressure) * moving)
    return jnp.stack(pieces)


def rusanov(left_state, right_state, left_flux, right_flux, left_speed, right_speed):
    biggest = jnp.maximum(left_speed, right_speed)
    return 0.5 * (left_flux + right_flux) - 0.5 * biggest * (right_state - left_state)


def advance(extended):
    velocity, pressure, sound_speed = cell_values(extended)
    cell_flux = physical_flux(extended, velocity, pressure, 0)
    cell_speed = jnp.abs(velocity[0]) + sound_speed
    face_flux = rusanov(
        extended[:, :-1],
        extended[:, 1:],
        cell_flux[:, :-1],
        cell_flux[:, 1:],
        cell_speed[:-1],
        cell_speed[1:],
    )
    interior = extended[:, 1:-1]
    change = face_flux[:, 1:] - face_flux[:, :-1]
    inner_velocity = velocity[:, 1:-1]
    inner_pressure = pressure[1:-1]
    inner_sound = sound_speed[1:-1]
    for normal in (1, 2):
        side_flux = physical_flux(interior, inner_velocity, inner_pressure, normal)
        side_speed = jnp.abs(inner_velocity[normal]) + inner_sound
        grid_axis = normal + 1
        face_values = rusanov(
            interior,
            jnp.roll(interior, -1, grid_axis),
            side_flux,
            jnp.roll(side_flux, -1, grid_axis),
            side_speed,
            jnp.roll(side_speed, -1, normal),
        )
        change = change + (face_values - jnp.roll(face_values, 1, grid_axis))
    return (interior - time_step * change, face_flux)


def on_device(fine_state, patch_ghosts, coarse_state, coarse_face_term, dest_grp, dest_column):
    box_count = lax.axis_size("box")
    box_place = lax.axis_index("box")
    at_low = box_place == 0
    at_high = box_place == box_count - 1
    current = fine_state[0]
    ghosts = patch_ghosts[0]
    fields, cells_along, cells_across, cells_depth = current.shape

    def with_ghosts(extended, width, time_frac):
        ghost_low = (1.0 - time_frac) * ghosts[0, 0] + time_frac * ghosts[1, 0]
        ghost_high = (1.0 - time_frac) * ghosts[0, 1] + time_frac * ghosts[1, 1]
        edge_shape = (fields, width, cells_across, cells_depth)
        lower = jnp.where(
            at_low, jnp.broadcast_to(ghost_low[:, None], edge_shape), extended[:, :width]
        )
        upper = jnp.where(
            at_high, jnp.broadcast_to(ghost_high[:, None], edge_shape), extended[:, -width:]
        )
        return jnp.concatenate([lower, extended[:, width:-width], upper], axis=1)

    extended = extended_2(current, (("box", 1),), 2)
    halfway, first_flux = advance(with_ghosts(extended, 2, 0.0))
    updated, second_flux = advance(with_ghosts(halfway, 1, 0.5))
    low_sum = first_flux[:, 1] + second_flux[:, 0]
    high_sum = first_flux[:, -2] + second_flux[:, -1]
    coarse_rows = cells_along // 2
    coarse_cols = cells_across // 2
    coarse_depth = cells_depth // 2
    averaged = updated.reshape(fields, coarse_rows, 2, coarse_cols, 2, coarse_depth, 2).mean(
        axis=(2, 4, 6)
    )
    avg_records = averaged.transpose(1, 2, 0, 3).reshape(
        coarse_rows * coarse_cols, fields, coarse_depth
    )
    face_sum = jnp.where(at_low, low_sum, high_sum)
    face_coarse = (
        face_sum.reshape(fields, coarse_cols, 2, coarse_depth, 2)
        .sum(axis=(2, 4))
        .transpose(1, 0, 2)
    )
    flux_records = jnp.where(at_low, -time_step / 8, time_step / 8) * face_coarse
    records = jnp.concatenate([avg_records, flux_records], axis=0)
    count_average = coarse_rows * coarse_cols
    total = count_average + coarse_cols
    is_live = jnp.concatenate(
        [jnp.ones((count_average,), bool), jnp.broadcast_to(at_low | at_high, (coarse_cols,))]
    )
    kind_sign = jnp.concatenate(
        [jnp.ones((count_average,), jnp.float32), -jnp.ones((coarse_cols,), jnp.float32)]
    )
    owners = dest_grp[0, 0]
    columns = dest_column[0, 0]
    group_count = lax.axis_size("grp")
    capacity = (total + group_count - 1) // group_count
    record_ids = jnp.arange(total, dtype=jnp.int32)
    same_owner = owners[:, None] == owners[None, :]
    earlier = record_ids[None, :] < record_ids[:, None]
    position = jnp.sum((same_owner & earlier).astype(jnp.int32), axis=1)
    slot_code = jnp.where(is_live, (columns + 1).astype(jnp.float32) * kind_sign, 0.0)
    outgoing = (
        jnp.zeros((group_count, capacity, fields, coarse_depth), jnp.float32)
        .at[owners, position]
        .set(records)
    )
    out_codes = jnp.zeros((group_count, capacity), jnp.float32).at[owners, position].set(slot_code)
    incoming, in_codes = (
        lax.all_to_all(outgoing, "grp", split_axis=0, concat_axis=0, tiled=True),
        lax.all_to_all(out_codes, "grp", split_axis=0, concat_axis=0, tiled=True),
    )
    flat = incoming.reshape(group_count * capacity, fields * coarse_depth)
    codes = in_codes.reshape(group_count * capacity)
    targets = (record_ids + 1).astype(jnp.float32)
    avg_hot = (codes[None, :] == targets[:, None]).astype(jnp.float32)
    face_hot = (codes[None, :] == -targets[:, None]).astype(jnp.float32)
    values = jnp.dot(
        avg_hot + face_hot,
        flat,
        precision=lax.Precision.HIGHEST,
        preferred_element_type=jnp.float32,
    ).reshape(total, fields, coarse_depth)
    avg_flag = jnp.sum(avg_hot, axis=1)
    face_flag = jnp.sum(face_hot, axis=1)
    coarse_new = jnp.where(
        avg_flag[:, None, None] > 0,
        values,
        coarse_state[0, 0] + face_flag[:, None, None] * (values - coarse_face_term[0, 0]),
    )
    return (updated[None], coarse_new[None, None])


def solution(mesh):
    in_specs = (
        P("grp", None, "box", None, None),
        P("grp", None, None, None, None, None),
        P("grp", "box", None, None, None),
        P("grp", "box", None, None, None),
        P("grp", "box", None),
        P("grp", "box", None),
    )
    out_specs = (P("grp", None, "box", None, None), P("grp", "box", None, None, None))
    return jax.shard_map(
        on_device, mesh=mesh, in_specs=in_specs, out_specs=out_specs, check_vma=False
    )
```

profile of v0, /device:TPU:0, one launch (start us, length us, event | category | flops | bytes accessed | tf_op | source)
XLA Modules:
  0.0 66.8 jit_solution(11364599939020816450)
XLA Ops:
  0.6 0.9 %convert_reduce_fusion.2 = s32[24]{0:T(128)S(1)} fusion(s32[24]{0:T(128)} %bitcast.224), kind=kLoop, calls=%fused_computation.166 | loop fusion | flops 2856 | bytes 192 | tf_op jit(solution)/shard_map/reduce_sum | solution.py:144
  1.5 0.7 fusion.71
  2.2 0.7 %pad_select_fusion = f32[24]{0:T(128)S(1)} fusion(pred[16]{0:T(512)(128)(4,1)S(1)} %broadcast.166, pred[]{:T(512)S(6)} %or.5, f32[1,1,24]{2,1,0:T(1,128)} %constant.26.clone.1, s32[1,1,24]{2,1,0:T(1,128)} %param.11), kind=kLoop, calls=%fused_computation.175 | loop fusion | flops 96 | bytes 305 | tf_op jit(solution)/shard_map/jit(_where)/select_n | solution.py:145
  2.9 2.0 %scatter_fusion = f32[16,2]{0,1:T(2,128)S(1)} fusion(f32[16,2]{0,1:T(2,128)S(1)} %broadcast_in_dim.24, s32[24]{0:T(128)S(1)} %fusion.71, f32[24]{0:T(128)S(1)} %pad_select_fusion), kind=kCustom, calls=%fused_computation | custom fusion | bytes 480 | tf_op jit(solution)/shard_map/scatter | solution.py:151
  4.9 0.7 %copy.47 = f32[16,1,2]{2,1,0:T(1,128)} copy(f32[16,1,2]{0,2,1:T(2,128)S(1)} %bitcast.208) | data formatting | bytes 256 | tf_op jit(solution)/shard_map/all_to_all | solution.py:154
  5.6 8.3 %all-to-all-start = ((f32[16,1,2]{2,1,0:T(1,128)}), f32[16,1,2]{2,1,0:T(1,128)S(1)}, u32[]{:S(2)}, u32[]{:S(2)}) async-start(f32[16,1,2]{2,1,0:T(1,128)} %copy.47), calls=%async_computation | async-start | bytes 16384 | tf_op jit(solution)/shard_map/all_to_all | solution.py:154
  14.0 1.0 %fusion.73 = (f32[5,2,16,256]{3,2,1,0:T(8,128)S(1)}, f32[5,2,16,256]{3,2,1,0:T(8,128)S(1)}) fusion(f32[5,4,16,256]{3,2,1,0:T(8,128)} %bitcast.216), kind=kLoop, calls=%fused_computation.183 | loop fusion | bytes 655360 | tf_op jit(solution)/shard_map/slice | solution.py:15
  15.0 1.5 %collective-permute-start = (f32[5,2,16,256]{3,2,1,0:T(8,128)S(1)}, f32[5,2,16,256]{3,2,1,0:T(8,128)S(1)}, u32[]{:S(2)}, u32[]{:S(2)}) collective-permute-start(f32[5,2,16,256]{3,2,1,0:T(8,128)S(1)} %get-tuple-element.44), channel_id=1, source_target_pairs={{0,1},{2,3},{4,5},{6,7},{8,9},{10,11},{12,13},{14,15},{16,17},{18,... | collective-permute-start | bytes 491528 | tf_op jit(solution)/shard_map/ppermute | solution.py:18
  16.5 1.3 %collective-permute-start.1 = (f32[5,2,16,256]{3,2,1,0:T(8,128)S(1)}, f32[5,2,16,256]{3,2,1,0:T(8,128)S(1)}, u32[]{:S(2)}, u32[]{:S(2)}) collective-permute-start(f32[5,2,16,256]{3,2,1,0:T(8,128)S(1)} %get-tuple-element.45), channel_id=1, source_target_pairs={{1,0},{3,2},{5,4},{7,6},{9,8},{11,10},{13,12},{15,14},{17,16},{19,... | collective-permute-start | bytes 491528 | tf_op jit(solution)/shard_map/ppermute | solution.py:20
  17.8 0.0 copy-start.1
  17.8 1.1 %add_bitcast_fusion.1 = (f32[5,16,256]{2,1,0:T(8,128)S(1)}, f32[5,16,256]{2,1,0:T(8,128)S(1)}) fusion(f32[2,2,5,16,256]{4,3,2,1,0:T(8,128)} %bitcast.220), kind=kLoop, calls=%fused_computation.129 | loop fusion | flops 81920 | bytes 491520 | tf_op jit(solution)/shard_map/add | solution.py:96
  18.9 2.3 %all-to-all-done = f32[16,1,2]{2,1,0:T(1,128)S(1)} async-done(((f32[16,1,2]{2,1,0:T(1,128)}), f32[16,1,2]{2,1,0:T(1,128)S(1)}, u32[]{:S(2)}, u32[]{:S(2)}) %all-to-all-start) | async-done | bytes 160 | tf_op jit(solution)/shard_map/all_to_all | solution.py:154
  21.2 0.5 broadcast.234
  21.7 0.7 %reduce.3 = f32[16,2]{1,0:T(8,128)S(1)} reduce(f32[16,1,2]{2,1,0:T(1,128)S(1)} %all-to-all-done, f32[]{:T(128)} %broadcast.234), dimensions={1}, to_apply=%all_to_all.10.reduce_sub_computation.3 | reduce | bytes 260 | tf_op jit(solution)/shard_map/all_to_all | solution.py:154
  22.4 0.1 eq.53
  22.5 0.2 convert_reduce_fusion.1
  22.6 0.0 collective-permute-done
  22.7 0.0 collective-permute-done.1
  22.7 1.0 %pad_maximum_fusion = f32[5,8,16,256]{3,2,1,0:T(8,128)S(1)} fusion(f32[5,2,16,256]{3,2,1,0:T(8,128)S(1)} %broadcast_select_fusion, f32[5,4,16,256]{3,2,1,0:T(8,128)} %bitcast.217, f32[5,2,16,256]{3,2,1,0:T(8,128)S(1)} %broadcast_select_fusion.1), kind=kLoop, calls=%fused_computation.2 | loop fusion | flops 327680 | bytes 1310720 | tf_op jit(solution)/shard_map/concatenate | solution.py:105
  23.9 0.2 slice.483
  24.1 0.1 multiply_reduce_fusion
  24.2 0.1 bitcast_add_fusion
  24.3 0.1 slice.481
  24.6 0.2 slice.479
  24.9 0.0 copy-start.3
  25.1 0.1 fusion.35
  25.2 0.0 copy-done.1
  25.2 0.5 fusion.13
  25.7 0.1 slice.485
  25.8 0.2 fusion.1
  26.0 0.4 fusion.10
  26.4 0.0 copy-done.3
  26.5 0.1 slice.523
  26.9 0.1 bitcast_add_fusion.1
  27.0 0.1 slice.521
  27.2 0.1 slice.519
  27.6 0.1 fusion.16
  27.7 0.7 fusion.45
  28.3 0.1 fusion.51
  28.4 0.3 fusion.26
  28.8 0.0 copy-start
  28.8 0.7 %copy-done = f32[5,4,16,256]{3,2,1,0:T(8,128)} copy-done((f32[5,4,16,256]{3,2,1,0:T(8,128)}, f32[5,4,16,256]{3,2,1,0:T(8,128)S(1)}, u32[]{:S(2)}) %copy-start) | copy-done | bytes 327704
  29.5 0.1 slice.525
  29.6 1.5 %copy.50 = f32[5,1,16,256]{0,3,2,1:T(8,128)S(1)} copy(f32[5,1,16,256]{3,2,1,0:T(8,128)} %fusion.45) | data formatting | bytes 163840 | tf_op jit(solution)/shard_map/jit(_where)/select_n | solution.py:121
  31.2 2.9 %reduce_sum.71 = f32[5,8,128]{0,2,1:T(8,128)} reduce(f32[5,8,2,128,2]{0,4,3,2,1:T(2,128)S(1)} %bitcast.210, f32[]{:T(128)} %constant.17.clone.1), dimensions={2,4}, to_apply=%region_6.7 | reduce | flops 15360 | bytes 102404 | tf_op jit(solution)/shard_map/reduce_sum | solution.py:124
  34.1 1.1 %multiply_bitcast_fusion = f32[8,5,128]{1,2,0:T(8,128)S(1)} fusion(f32[5,8,128]{0,2,1:T(8,128)} %reduce_sum.71, f32[]{:T(128)S(6)} %select_n.87), kind=kLoop, calls=%fused_computation.8 | loop fusion | flops 5120 | bytes 40964 | tf_op jit(solution)/shard_map/mul | solution.py:127
  35.2 0.2 copy.52
  35.4 1.3 %fusion.21 = f32[5,4,16,256]{3,2,1,0:T(8,128)S(1)} fusion(f32[5,5,16,256]{3,2,1,0:T(8,128)S(1)} %fusion.16, f32[5,4,16,256]{3,2,1,0:T(8,128)} %copy-done, f32[5,4,15,256]{3,2,1,0:T(8,128)} %bitcast.215, f32[5,4,1,256]{3,2,1,0:T(1,128)S(1)} %slice.516, f32[5,4,16,256]{3,2,1,0:T(8,128)S(1)} %get-tuple-element.34, f32[5,4,16,255]{3,2,1,0:T(8,128)S(1)} %bitcast.214, ...), kind=kLoop, calls=%fused_computation.42 | loop fusion | flops 737280 | bytes 2621440 | tf_op jit(solution)/shard_map/sub | solution.py:83
  36.7 0.0 copy-start.2
  36.7 4.9 %copy.48 = f32[5,4,16,256]{0,3,2,1:T(8,128)} copy(f32[5,4,16,256]{3,2,1,0:T(8,128)S(1)} %fusion.21) | data formatting | bytes 655360 | tf_op jit(solution)/shard_map/sub | solution.py:83
  41.6 0.0 copy-start.4
  41.6 0.0 copy-start.5
  41.6 8.8 %reduce_sum.70 = f32[5,2,8,128]{0,3,2,1:T(8,128)S(1)} reduce(f32[5,2,2,8,2,128,2]{0,6,5,4,3,2,1:T(2,128)} %bitcast.209, f32[]{:T(128)} %constant.17.clone.1), dimensions={2,4,6}, to_apply=%region_5.6 | reduce | flops 71680 | bytes 368644 | tf_op jit(solution)/shard_map/reduce_sum | solution.py:115
  50.4 0.0 copy-done.2
  50.4 0.1 broadcast_multiply_fusion
  50.5 0.3 copy.51
  50.8 1.9 %scatter_fusion.1 = f32[16,2,5,128]{3,2,1,0:T(8,128)S(1)} fusion(f32[16,2,5,128]{3,2,1,0:T(8,128)S(1)} %broadcast_in_dim.27, s32[24]{0:T(128)S(1)} %fusion.71, f32[24,5,128]{2,1,0:T(8,128)S(1)} %pad_maximum_fusion.4), kind=kCustom, calls=%fused_computation.1 | custom fusion | bytes 184512 | tf_op jit(solution)/shard_map/scatter | solution.py:149
  52.8 0.7 %copy.53 = f32[16,2,5,128]{3,1,2,0:T(2,128)} copy(f32[16,2,5,128]{3,2,1,0:T(8,128)S(1)} %scatter_fusion.1) | data formatting | bytes 163840 | tf_op jit(solution)/shard_map/scatter | solution.py:149
  53.4 4.4 %all-to-all-start.1 = ((f32[16,2,5,128]{3,1,2,0:T(2,128)}), f32[16,2,5,128]{3,1,2,0:T(2,128)S(1)}, u32[]{:S(2)}, u32[]{:S(2)}) async-start(f32[16,2,5,128]{3,1,2,0:T(2,128)} %copy.53), calls=%async_computation.1 | async-start | bytes 163840 | tf_op jit(solution)/shard_map/all_to_all | solution.py:153
  57.9 7.9 %all-to-all-done.1 = f32[16,2,5,128]{3,1,2,0:T(2,128)S(1)} async-done(((f32[16,2,5,128]{3,1,2,0:T(2,128)}), f32[16,2,5,128]{3,1,2,0:T(2,128)S(1)}, u32[]{:S(2)}, u32[]{:S(2)}) %all-to-all-start.1) | async-done | bytes 81952 | tf_op jit(solution)/shard_map/all_to_all | solution.py:153
  65.8 0.0 copy-done.4
  65.8 0.0 copy-done.5
  65.9 0.9 %fusion.61 = f32[1,1,24,5,128]{4,2,3,1,0:T(8,128)} fusion(f32[1,1,24,5,128]{4,2,3,1,0:T(8,128)S(1)} %copy-done.4, f32[1,1,24,5,128]{4,2,3,1,0:T(8,128)S(1)} %copy-done.5, f32[24]{0:T(128)S(1)} %get-tuple-element.3, pred[24]{0:T(512)(128)(4,1)S(1)} %broadcast_compare_fusion, f32[32]{0:T(128)S(1)} %eq.53, f32[24]{0:T(128)S(1)} %fusion.72, ...), kind=kOutput, calls=%fused_computation.161 | convolution fusion | flops 5963520 | bytes 266680 | tf_op jit(solution)/shard_map/dot_general | solution.py:161
  (61 shorter events, 1.2 us)
Async XLA Ops:
  5.6 15.6 %all-to-all-start = ((f32[16,1,2]{2,1,0:T(1,128)}), f32[16,1,2]{2,1,0:T(1,128)S(1)}, u32[]{:S(2)}, u32[]{:S(2)}) async-start(f32[16,1,2]{2,1,0:T(1,128)} %copy.47), calls=%async_computation | async-start | bytes 16384 | tf_op jit(solution)/shard_map/all_to_all | solution.py:154
  15.0 7.7 %collective-permute-start = (f32[5,2,16,256]{3,2,1,0:T(8,128)S(1)}, f32[5,2,16,256]{3,2,1,0:T(8,128)S(1)}, u32[]{:S(2)}, u32[]{:S(2)}) collective-permute-start(f32[5,2,16,256]{3,2,1,0:T(8,128)S(1)} %get-tuple-element.44), channel_id=1, source_target_pairs={{0,1},{2,3},{4,5},{6,7},{8,9},{10,11},{12,13},{14,15},{16,17},{18,... | collective-permute-start | bytes 491528 | tf_op jit(solution)/shard_map/ppermute | solution.py:18
  16.5 6.2 %collective-permute-start.1 = (f32[5,2,16,256]{3,2,1,0:T(8,128)S(1)}, f32[5,2,16,256]{3,2,1,0:T(8,128)S(1)}, u32[]{:S(2)}, u32[]{:S(2)}) collective-permute-start(f32[5,2,16,256]{3,2,1,0:T(8,128)S(1)} %get-tuple-element.45), channel_id=1, source_target_pairs={{1,0},{3,2},{5,4},{7,6},{9,8},{11,10},{13,12},{15,14},{17,16},{19,... | collective-permute-start | bytes 491528 | tf_op jit(solution)/shard_map/ppermute | solution.py:20
  17.8 7.4 %copy-start.1 = (f32[1,5,4,16,256]{4,3,2,1,0:T(8,128)S(1)}, f32[1,5,4,16,256]{4,3,2,1,0:T(8,128)}, u32[]{:S(2)}) copy-start(f32[1,5,4,16,256]{4,3,2,1,0:T(8,128)} %param.6) | copy-start | bytes 983044
  24.9 1.5 %copy-start.3 = (f32[1,2,2,5,16,256]{5,4,3,2,1,0:T(8,128)S(1)}, f32[1,2,2,5,16,256]{5,4,3,2,1,0:T(8,128)}, u32[]{:S(2)}) copy-start(f32[1,2,2,5,16,256]{5,4,3,2,1,0:T(8,128)} %param.7) | copy-start | bytes 983044
  28.8 0.7 %copy-start = (f32[5,4,16,256]{3,2,1,0:T(8,128)}, f32[5,4,16,256]{3,2,1,0:T(8,128)S(1)}, u32[]{:S(2)}) copy-start(f32[5,4,16,256]{3,2,1,0:T(8,128)S(1)} %get-tuple-element.35) | copy-start | bytes 983044
  36.7 13.7 %copy-start.2 = (f32[5,4,16,256]{3,2,1,0:T(8,128)}, f32[5,4,16,256]{3,2,1,0:T(8,128)S(1)}, u32[]{:S(2)}) copy-start(f32[5,4,16,256]{3,2,1,0:T(8,128)S(1)} %fusion.21) | copy-start | bytes 983044
  41.6 24.2 %copy-start.4 = (f32[1,1,24,5,128]{4,2,3,1,0:T(8,128)S(1)}, f32[1,1,24,5,128]{4,2,3,1,0:T(8,128)}, u32[]{:S(2)}) copy-start(f32[1,1,24,5,128]{4,2,3,1,0:T(8,128)} %param.9) | copy-start | bytes 184324
  41.6 24.2 %copy-start.5 = (f32[1,1,24,5,128]{4,2,3,1,0:T(8,128)S(1)}, f32[1,1,24,5,128]{4,2,3,1,0:T(8,128)}, u32[]{:S(2)}) copy-start(f32[1,1,24,5,128]{4,2,3,1,0:T(8,128)} %param.8) | copy-start | bytes 184324
  53.4 12.4 %all-to-all-start.1 = ((f32[16,2,5,128]{3,1,2,0:T(2,128)}), f32[16,2,5,128]{3,1,2,0:T(2,128)S(1)}, u32[]{:S(2)}, u32[]{:S(2)}) async-start(f32[16,2,5,128]{3,1,2,0:T(2,128)} %copy.53), calls=%async_computation.1 | async-start | bytes 163840 | tf_op jit(solution)/shard_map/all_to_all | solution.py:153
where the time goes:
time: 67.3 us; the launch traced here: 66.8 us
  other arithmetic  22.7 us (34%)
  local copies, waits for them, and re-layouts  16 us (24%)
  starting transfers between devices  15.5 us (23%)
  waiting for transfers between devices  10.2 us (15%)
  between operations  1.36 us (2%)
  matrix products  0.9 us (1%)
    reduce_sum x1, other arithmetic, on_device(): updated.reshape(fields, coarse_rows, 2, coarse_cols, 2, coarse_depth, 2)  8.76 us
    all_to_all x1, starting transfers between devices, on_device(): lax.all_to_all(out_codes, 'grp', split_axis=0, concat_axis=0, tiled=True)  8.34 us
    all_to_all x1, waiting for transfers between devices, on_device(): lax.all_to_all(outgoing, 'grp', split_axis=0, concat_axis=0, tiled=True)  7.91 us
    sub x1, local copies, waits for them, and re-layouts, advance(): return (interior - time_step * change, face_flux)  4.91 us
    all_to_all x1, starting transfers between devices, on_device(): lax.all_to_all(outgoing, 'grp', split_axis=0, concat_axis=0, tiled=True)  4.45 us
    reduce_sum x1, other arithmetic, on_device(): face_coarse = face_sum.reshape(fields, coarse_cols, 2, coarse_depth, 2).s...  2.93 us
    scatter x2, local copies, waits for them, and re-layouts, on_device(): outgoing = jnp.zeros((group_count, capacity, fields, coarse_depth), jnp.f...  2.57 us
    all_to_all x1, waiting for transfers between devices, on_device(): lax.all_to_all(out_codes, 'grp', split_axis=0, concat_axis=0, tiled=True)  2.3 us
  transfers between devices with their start and end apart: 4, of which 2 were waited for; matrix products, arithmetic and copies ran while one was open for 5% of the time, Pallas kernels for 0%

commit v1 on v0

v1 whole, which is shorter than its diff:
```python
import functools

import jax
import jax.numpy as jnp
from jax import lax
from jax.experimental import pallas as pl
from jax.experimental.pallas import tpu as pltpu
from jax.sharding import PartitionSpec as P

gamma_ratio = 1.4
time_step = 0.06
vmem_limit = 8 * 1024 * 1024


def split_dot(lhs, rhs, split_lhs, dims=(((1,), (0,)), ((), ()))):
    data = lhs if split_lhs else rhs
    exact = (rhs if split_lhs else lhs).astype(jnp.bfloat16)
    total = None
    for _ in range(3):
        term = data.astype(jnp.bfloat16)
        data = data - term.astype(jnp.float32)
        pair = (term, exact) if split_lhs else (exact, term)
        part = lax.dot_general(*pair, dims, preferred_element_type=jnp.float32)
        total = part if total is None else total + part
    return total


def next_z(values):
    return pltpu.roll(values, values.shape[-1] - 1, 1)


def last_z(values):
    return pltpu.roll(values, 1, 1)


def next_y(pair):
    even, odd = pair
    return (odd, pltpu.roll(even, even.shape[0] - 1, 0))


def last_y(pair):
    even, odd = pair
    return (pltpu.roll(odd, 1, 0), even)


def both(function, *pairs):
    return tuple(function(*halves) for halves in zip(*pairs))


class Cells:

    def __init__(self, state):
        density, mom = state[0], state[1:4]
        inverse = both(lambda d: 1.0 / d, density)
        velocity = [both(lambda m, r: m * r, m, inverse) for m in mom]
        square = {}
        for i in range(3):
            for j in range(i, 3):
                square[i, j] = both(lambda m, v: m * v, mom[i], velocity[j])
        pressure = both(
            lambda e, a, b, c: (gamma_ratio - 1.0) * (e - 0.5 * (a + b + c)),
            state[4], square[0, 0], square[1, 1], square[2, 2],
        )
        sound = both(lambda p, r: jnp.sqrt(gamma_ratio * p * r), pressure, inverse)
        enthalpy = both(jnp.add, state[4], pressure)
        self.state = state
        self.flux = []
        self.speed = []
        for normal in range(3):
            pieces = [mom[normal]]
            for member in range(3):
                term = square[min(member, normal), max(member, normal)]
                pieces.append(both(jnp.add, term, pressure) if member == normal else term)
            pieces.append(both(jnp.multiply, enthalpy, velocity[normal]))
            self.flux.append(pieces)
            self.speed.append(both(lambda v, c: jnp.abs(v) + c, velocity[normal], sound))


def doubled_face(left_state, right_state, left_flux, right_flux, left_speed, right_speed):
    biggest = both(jnp.maximum, left_speed, right_speed)
    return [
        both(lambda a, b, f, g, s: (f + g) - s * (b - a), ls, rs, lf, rf, biggest)
        for ls, rs, lf, rf in zip(left_state, right_state, left_flux, right_flux)
    ]


def x_face(left, right):
    return doubled_face(
        left.state, right.state, left.flux[0], right.flux[0], left.speed[0], right.speed[0]
    )


def side_change(cells):
    change = [None] * len(cells.state)
    for normal in (1, 2):
        if normal == 1:
            ahead, behind = next_y, last_y
        else:
            ahead = functools.partial(both, next_z)
            behind = functools.partial(both, last_z)
        faces = doubled_face(
            cells.state, [ahead(s) for s in cells.state],
            cells.flux[normal], [ahead(f) for f in cells.flux[normal]],
            cells.speed[normal], ahead(cells.speed[normal]),
        )
        for index, face in enumerate(faces):
            part = both(jnp.subtract, face, behind(face))
            change[index] = part if change[index] is None else both(jnp.add, change[index], part)
    return change


def advance(layers, on_update, on_face):
    before, low_face, change = Cells(layers[0]()), None, None
    for index in range(1, len(layers)):
        here = Cells(layers[index]())
        face = x_face(before, here)
        on_face(index - 1, face)
        if index >= 2:
            half = 0.5 * time_step
            on_update(
                index - 1,
                [
                    both(lambda u, c, h, l: u - half * (c + (h - l)), u, c, h, l)
                    for u, c, h, l in zip(before.state, change, face, low_face)
                ],
            )
        if index < len(layers) - 1:
            change = side_change(here)
        before, low_face = here, face


def one_hot_slots(owners, groups, capacity):
    total = owners.shape[1]
    hit = owners == lax.broadcasted_iota(jnp.int32, (groups, total), 0)
    hot = jnp.where(hit, 1.0, 0.0)
    earlier = (
        lax.broadcasted_iota(jnp.int32, (total, total), 0)
        < lax.broadcasted_iota(jnp.int32, (total, total), 1)
    )
    rank = jnp.dot(
        hot.astype(jnp.bfloat16),
        jnp.where(earlier, 1.0, 0.0).astype(jnp.bfloat16),
        preferred_element_type=jnp.float32,
    )
    return [jnp.where(hit & (rank == float(slot)), 1.0, 0.0) for slot in range(capacity)]


def patch_kernel(
    box_count, groups, capacity, rows,
    box_ref, fine_ref, ghost_ref, low_ref, high_ref, owner_ref, column_ref,
    new_ref, out_ref, half_ref, stage_ref,
):
    box_place = box_ref[0]
    at_low = box_place == 0
    at_high = box_place == box_count - 1
    fields, along, across, depth = fine_ref.shape
    half_across = across // 2
    lanes = stage_ref.shape[-1]
    pieces = depth // lanes
    mirrored = box_count == 2
    side = jnp.where(at_high, 1, 0) if mirrored else 0
    turn = jnp.where(at_high, -1.0, 1.0)

    def place(index):
        return jnp.where(at_high, along - 1 - index, index) if mirrored else index

    def oriented(field, values):
        return turn * values if mirrored and field == 1 else values

    slots = iter(range(stage_ref.shape[0]))

    def parted(planes):
        slot = next(slots)
        for f, plane in enumerate(planes):
            for piece in range(pieces):
                stage_ref[slot, f, piece] = oriented(f, plane[:, piece * lanes:(piece + 1) * lanes])
        return [
            tuple(
                jnp.concatenate(
                    [
                        stage_ref[slot, f, piece, pl.ds(parity, half_across, stride=2), :]
                        for piece in range(pieces)
                    ],
                    axis=1,
                )
                for parity in (0, 1)
            )
            for f in range(fields)
        ]

    def rows_of(ref, layer):
        return parted([ref[f, layer] for f in range(fields)])

    def ghost_layer(at, time_frac):
        if time_frac == 0.0:
            return parted([ghost_ref[0, at, f] for f in range(fields)])
        return parted(
            [
                (1.0 - time_frac) * ghost_ref[0, at, f] + time_frac * ghost_ref[1, at, f]
                for f in range(fields)
            ]
        )

    def half_layer(index):
        return [tuple(half_ref[index, f, parity] for parity in (0, 1)) for f in range(fields)]

    def picked(flag, first, second):
        return [both(lambda a, b: jnp.where(flag, a, b), a, b) for a, b in zip(first, second)]

    def fine_layer(index):
        return rows_of(fine_ref, place(index))

    inner = [functools.partial(fine_layer, index) for index in range(along)]
    low_faces, high_faces = [], []
    if mirrored:
        start = 0
        first = [lambda: ghost_layer(side, 0.0), *inner]
        first += [lambda: rows_of(low_ref, place(0)), lambda: rows_of(low_ref, place(1))]
        second = [lambda: ghost_layer(side, 0.5)]
        second += [functools.partial(half_layer, index) for index in range(along + 1)]
        low_at = (0, 0)
        high_at = (-1, -1)
    else:
        start = 1
        width = low_ref.shape[1]
        first = [lambda: rows_of(low_ref, width - 2)]
        first += [
            lambda: picked(at_low, ghost_layer(0, 0.0), rows_of(low_ref, width - 1)),
            *inner,
            lambda: picked(at_high, ghost_layer(1, 0.0), rows_of(high_ref, 0)),
            lambda: rows_of(high_ref, 1),
        ]
        second = [lambda: picked(at_low, ghost_layer(0, 0.5), half_layer(0))]
        second += [functools.partial(half_layer, 1 + index) for index in range(along)]
        second += [lambda: picked(at_high, ghost_layer(1, 0.5), half_layer(along + 1))]
        low_at = (1, 0)
        high_at = (along + 1, along)

    def keep_half(index, state):
        for f in range(fields):
            for parity in (0, 1):
                half_ref[index - 1, f, parity] = state[f][parity]

    sums = {}

    def keep_new(index, state):
        slot = next(slots)
        layer = place(index - 1)
        for f in range(fields):
            for piece in range(pieces):
                part = slice(piece * lanes, (piece + 1) * lanes)
                for parity in (0, 1):
                    stage_ref[slot, f, piece, pl.ds(parity, half_across, stride=2), :] = oriented(
                        f, state[f][parity][:, part]
                    )
                new_ref[f, layer, :, part] = stage_ref[slot, f, piece]
            pooled = state[f][0] + state[f][1]
            key = (f, (index - 1) // 2)
            sums[key] = sums[key] + pooled if key in sums else pooled

    def face_keeper(step):
        def keep(index, face):
            if index == low_at[step]:
                low_faces.append(face)
            if index == high_at[step]:
                high_faces.append(face)
        return keep

    advance(first, keep_half, face_keeper(0))
    advance(second, keep_new, face_keeper(1))

    planes = along // 2
    blocks = []
    for f in range(fields):
        for plane in range(planes):
            if mirrored:
                value = jnp.where(at_high, sums[f, planes - 1 - plane], sums[f, plane])
            else:
                value = sums[f, plane]
            blocks.append(oriented(f, 0.125 * value))
        low = [sum(halves) for halves in zip(*(step[f] for step in low_faces))]
        face_sum = low[0] + low[1]
        if not mirrored:
            high = [sum(halves) for halves in zip(*(step[f] for step in high_faces))]
            face_sum = jnp.where(at_low, face_sum, -(high[0] + high[1]))
        blocks.append(oriented(f, (-0.5 * time_step / 8) * face_sum))
    stacked = jnp.concatenate(blocks, axis=0)
    coarse_depth = depth // 2
    lane_pair = lax.broadcasted_iota(jnp.int32, (depth, coarse_depth), 0) // 2
    pool = jnp.where(
        lane_pair == lax.broadcasted_iota(jnp.int32, (depth, coarse_depth), 1), 1.0, 0.0
    )
    records = split_dot(stacked, pool, True)

    total = owner_ref.shape[1]
    count_average = planes * half_across
    selections = one_hot_slots(owner_ref[...], groups, capacity)
    wide = jnp.concatenate(
        [records[f * total:(f + 1) * total] for f in range(fields)], axis=1
    )
    chosen = split_dot(jnp.concatenate(selections, axis=0), wide, False)
    record_ids = lax.broadcasted_iota(jnp.int32, (1, total), 1)
    codes = (column_ref[...] + 1).astype(jnp.float32)
    face_code = -codes if mirrored else jnp.where(at_low | at_high, -codes, 0.0)
    codes = jnp.where(record_ids < count_average, codes, face_code)
    for slot in range(capacity):
        base = slot * (fields + 1)
        for f in range(fields):
            out_ref[pl.ds(base + f, groups, stride=rows), :] = chosen[
                slot * groups:(slot + 1) * groups, f * coarse_depth:(f + 1) * coarse_depth
            ]
        code = jnp.sum(selections[slot] * codes, axis=1, keepdims=True)
        out_ref[pl.ds(base + fields, groups, stride=rows), :] = jnp.broadcast_to(
            code, (groups, coarse_depth)
        )


def owner_kernel(groups, capacity, rows, in_ref, state_ref, term_ref, out_ref):
    fields, total, coarse_depth = state_ref.shape
    codes, values = [], []
    for slot in range(capacity):
        base = slot * (fields + 1)
        code = in_ref[pl.ds(base + fields, groups, stride=rows), :]
        codes.append(code)
        values.append(
            jnp.concatenate(
                [
                    jnp.where(code != 0.0, in_ref[pl.ds(base + f, groups, stride=rows), :], 0.0)
                    for f in range(fields)
                ],
                axis=1,
            )
        )
    codes = jnp.concatenate(codes, axis=0)
    values = jnp.concatenate(values, axis=0)
    count = codes.shape[0]
    across = jnp.transpose(codes)[:total]
    column = (lax.broadcasted_iota(jnp.int32, (total, count), 0) + 1).astype(jnp.float32)
    hot = jnp.where(jnp.abs(across) == column, 1.0, 0.0)
    kind = jnp.where(codes > 0.0, 1.0, jnp.where(codes < 0.0, -1.0, 0.0))
    flag = jnp.dot(
        hot.astype(jnp.bfloat16), kind.astype(jnp.bfloat16), preferred_element_type=jnp.float32
    )
    got = split_dot(hot, values, False)
    for f in range(fields):
        value = got[:, f * coarse_depth:(f + 1) * coarse_depth]
        state = state_ref[f]
        refluxed = state + (value - term_ref[f])
        out_ref[f] = jnp.where(flag > 0.0, value, jnp.where(flag < 0.0, refluxed, state))


def on_device(fine_state, patch_ghosts, coarse_state, coarse_face_term, dest_grp, dest_column):
    box_count = lax.axis_size("box")
    group_count = lax.axis_size("grp")
    box_place = lax.axis_index("box")
    current = fine_state[0]
    fields, cells_along, cells_across, cells_depth = current.shape
    total = dest_grp.shape[-1]
    capacity = (total + group_count - 1) // group_count
    rows = -(-capacity * (fields + 1) // 8) * 8
    coarse_depth = cells_depth // 2
    params = pltpu.CompilerParams(vmem_limit_bytes=vmem_limit)

    if box_count == 2:
        low = lax.ppermute(current, "box", [(0, 1), (1, 0)])
        high = low
    else:
        ends = box_count - 1
        low = lax.ppermute(current[:, -2:], "box", [(i, i + 1) for i in range(ends)])
        high = lax.ppermute(current[:, :2], "box", [(i + 1, i) for i in range(ends)])

    vmem = pl.BlockSpec(memory_space=pltpu.VMEM)
    halves = cells_along + (1 if box_count == 2 else 2)
    updated, outgoing = pl.pallas_call(
        functools.partial(patch_kernel, box_count, group_count, capacity, rows),
        out_shape=(
            jax.ShapeDtypeStruct(current.shape, jnp.float32),
            jax.ShapeDtypeStruct((group_count * rows, coarse_depth), jnp.float32),
        ),
        in_specs=[pl.BlockSpec(memory_space=pltpu.SMEM)] + [vmem] * 6,
        out_specs=(vmem, vmem),
        scratch_shapes=[
            pltpu.VMEM((halves, fields, 2, cells_across // 2, cells_depth), jnp.float32),
            pltpu.VMEM(
                (2 * cells_along + 8, fields, cells_depth // 128, cells_across, 128), jnp.float32
            ),
        ],
        compiler_params=params,
        name="patch",
    )(
        box_place.reshape(1), current, patch_ghosts[0], low, high,
        dest_grp[0], dest_column[0],
    )
    incoming = lax.all_to_all(
        outgoing.reshape(group_count, rows, coarse_depth),
        "grp", split_axis=0, concat_axis=0, tiled=True,
    ).reshape(group_count * rows, coarse_depth)
    coarse_new = pl.pallas_call(
        functools.partial(owner_kernel, group_count, capacity, rows),
        out_shape=jax.ShapeDtypeStruct((fields, total, coarse_depth), jnp.float32),
        in_specs=[vmem] * 3,
        out_specs=vmem,
        compiler_params=params,
        name="owner",
    )(
        incoming,
        coarse_state[0, 0].transpose(1, 0, 2),
        coarse_face_term[0, 0].transpose(1, 0, 2),
    )
    return (updated[None], coarse_new.transpose(1, 0, 2)[None, None])


def solution(mesh):
    in_specs = (
        P("grp", None, "box", None, None),
        P("grp", None, None, None, None, None),
        P("grp", "box", None, None, None),
        P("grp", "box", None, None, None),
        P("grp", "box", None),
        P("grp", "box", None),
    )
    out_specs = (P("grp", None, "box", None, None), P("grp", "box", None, None, None))
    return jax.shard_map(
        on_device, mesh=mesh, in_specs=in_specs, out_specs=out_specs, check_vma=False
    )
```

time: 67.3 us -> 24.2 us (0.36)
  other arithmetic: 22.7 us -> 0 us
  blocking collectives: 0 us -> 15.9 us
  starting transfers between devices: 15.5 us -> 0.56 us
  local copies, waits for them, and re-layouts: 16 us -> 2.62 us
  waiting for transfers between devices: 10.2 us -> 1.47 us
  Pallas kernels: 0 us -> 2.73 us
  matrix products: 0.9 us -> 0 us
  between operations: 1.36 us -> 0.64 us
    all_to_all x0 -> x1, blocking collectives: none -> 15.9 us  [on_device(): lax.all_to_all(outgoing.reshape(group_count, rows, coarse_depth), 'grp',...]
    reduce_sum x6 -> x0, other arithmetic: 12.9 us -> none  [the longest x1 8.76 us: on_device(): updated.reshape(fields, coarse_rows, 2, coarse_cols, 2, coarse_depth, 2)]
    all_to_all x2 -> x0, starting transfers between devices: 12.8 us -> none  [the longest x1 8.34 us: on_device(): lax.all_to_all(out_codes, 'grp', split_axis=0, concat_axis=0, tiled=True)]
    all_to_all x2 -> x0, waiting for transfers between devices: 10.2 us -> none  [the longest x1 7.91 us: on_device(): lax.all_to_all(outgoing, 'grp', split_axis=0, concat_axis=0, tiled=True)]
    sub x1 -> x0, local copies, waits for them, and re-layouts: 4.91 us -> none  [advance(): return (interior - time_step * change, face_flux)]
    scatter x3 -> x0, local copies, waits for them, and re-layouts: 4.59 us -> none  [the longest x2 2.57 us: on_device(): outgoing = jnp.zeros((group_count, capacity, fields, coarse_depth), jnp.f...]
    sub x6 -> x0, other arithmetic: 2.81 us -> none  [the longest x2 1.71 us: advance(): return (interior - time_step * change, face_flux)]
    pallas_call x0 -> x2, Pallas kernels: none -> 2.73 us  [the longest x1 1.87 us: on_device(): pl.pallas_call(functools.partial(patch_kernel, box_count, group_count, ca...]
  transfers between devices with their start and end apart: 4 -> 1, of which waited for: 2 -> 1; matrix products, arithmetic and copies ran while one was open for 5% -> 0% of each run, Pallas kernels for 0% -> 0%
where the time goes in v1:
time: 24.2 us; the launch traced here: 24 us
  blocking collectives  15.9 us (66%)
  Pallas kernels  2.73 us (11%)
  local copies, waits for them, and re-layouts  2.62 us (11%)
  waiting for transfers between devices  1.47 us (6%)
  between operations  0.64 us (3%)
  starting transfers between devices  0.56 us (2%)
    all_to_all x1, blocking collectives, on_device(): lax.all_to_all(outgoing.reshape(group_count, rows, coarse_depth), 'grp',...  15.9 us
    unnamed x12, local copies, waits for them, and re-layouts  2.62 us
    pallas_call x1, Pallas kernels, on_device(): pl.pallas_call(functools.partial(patch_kernel, box_count, group_count, ca...  1.87 us
    ppermute x1, waiting for transfers between devices, on_device(): low = lax.ppermute(current, 'box', [(0, 1), (1, 0)])  1.47 us
    pallas_call x1, Pallas kernels, on_device(): pl.pallas_call(functools.partial(owner_kernel, group_count, capacity, row...  0.87 us
    ppermute x1, starting transfers between devices, on_device(): low = lax.ppermute(current, 'box', [(0, 1), (1, 0)])  0.56 us
  transfers between devices with their start and end apart: 1, of which 1 were waited for; matrix products, arithmetic and copies ran while one was open for 0% of the time, Pallas kernels for 0%

profile of v1, /device:TPU:0, one launch (start us, length us, event | category | flops | bytes accessed | tf_op | source)
XLA Modules:
  0.0 24.0 jit_solution(3573067285970416880)
XLA Ops:
  0.6 0.6 %collective-permute-start = (f32[5,4,16,256]{3,2,1,0:T(8,128)}, f32[5,4,16,256]{3,2,1,0:T(8,128)S(1)}, u32[]{:S(2)}, u32[]{:S(2)}) collective-permute-start(f32[5,4,16,256]{3,2,1,0:T(8,128)} %bitcast.18), channel_id=1, source_target_pairs={{0,1},{1,0},{2,3},{3,2},{4,5},{5,4},{6,7},{7,6},{8,9},{9,8},{10,11... | collective-permute-start | bytes 983048 | tf_op jit(solution)/shard_map/ppermute | solution.py:365
  1.2 1.5 %collective-permute-done.low_ref.high_ref = f32[5,4,16,256]{3,2,1,0:T(8,128)S(1)} collective-permute-done((f32[5,4,16,256]{3,2,1,0:T(8,128)}, f32[5,4,16,256]{3,2,1,0:T(8,128)S(1)}, u32[]{:S(2)}, u32[]{:S(2)}) %collective-permute-start) | collective-permute-done | bytes 327712 | tf_op jit(solution)/shard_map/ppermute | solution.py:365
  2.7 0.0 copy-start.4
  2.7 0.0 copy-start.5
  2.7 0.7 %copy-done.4 = s32[1,1,24]{2,1,0:T(1,128)S(1)} copy-done((s32[1,1,24]{2,1,0:T(1,128)S(1)}, s32[1,1,24]{2,1,0:T(1,128)}, u32[]{:S(2)}) %copy-start.4) | copy-done | bytes 120
  3.3 0.0 copy-done.5
  3.3 0.0 copy-start
  3.3 1.0 %copy-done = f32[1,5,4,16,256]{4,3,2,1,0:T(8,128)S(1)} copy-done((f32[1,5,4,16,256]{4,3,2,1,0:T(8,128)S(1)}, f32[1,5,4,16,256]{4,3,2,1,0:T(8,128)}, u32[]{:S(2)}) %copy-start) | copy-done | bytes 327704
  4.3 0.0 copy-start.1
  4.3 1.0 %copy-done.1 = f32[1,2,2,5,16,256]{5,4,3,2,1,0:T(8,128)S(1)} copy-done((f32[1,2,2,5,16,256]{5,4,3,2,1,0:T(8,128)S(1)}, f32[1,2,2,5,16,256]{5,4,3,2,1,0:T(8,128)}, u32[]{:S(2)}) %copy-start.1) | copy-done | bytes 327704
  5.3 1.9 %patch.1 = (f32[5,4,16,256]{3,2,1,0:T(8,128)}, f32[256,128]{1,0:T(8,128)S(1)}) custom-call(s32[1]{0:T(128)} %bitcast.box_ref, f32[5,4,16,256]{3,2,1,0:T(8,128)S(1)} %bitcast.19, f32[2,2,5,16,256]{4,3,2,1,0:T(8,128)S(1)} %bitcast.20, f32[5,4,16,256]{3,2,1,0:T(8,128)S(1)} %collective-permute-done.low_ref.high_ref, ...), custom_call_target="tpu_custom_call" | custom-call | tf_op jit(solution)/shard_map/patch/pallas_call | solution.py:374
  7.1 0.0 copy-start.2
  7.1 0.0 copy-start.3
  7.1 15.9 %all_to_all.5 = f32[16,16,128]{2,1,0:T(8,128)S(1)} all-to-all(f32[16,16,128]{2,1,0:T(8,128)S(1)} %bitcast.21), channel_id=1, replica_groups=mesh['grp'=16,'box'=2] {'grp'}, dimensions={0} | all-to-all | bytes 262144 | tf_op jit(solution)/shard_map/all_to_all | solution.py:394
  23.1 0.0 copy-done.2
  23.1 0.0 copy-done.3
  23.1 0.9 %owner.1 = f32[5,24,128]{2,1,0:T(8,128)} custom-call(f32[256,128]{1,0:T(8,128)S(1)} %bitcast.17, f32[5,24,128]{2,1,0:T(8,128)S(1)} %bitcast.22, f32[5,24,128]{2,1,0:T(8,128)S(1)} %bitcast.23), custom_call_target="tpu_custom_call" | custom-call | tf_op jit(solution)/shard_map/owner/pallas_call | solution.py:398
Async XLA Ops:
  0.6 2.0 %collective-permute-start = (f32[5,4,16,256]{3,2,1,0:T(8,128)}, f32[5,4,16,256]{3,2,1,0:T(8,128)S(1)}, u32[]{:S(2)}, u32[]{:S(2)}) collective-permute-start(f32[5,4,16,256]{3,2,1,0:T(8,128)} %bitcast.18), channel_id=1, source_target_pairs={{0,1},{1,0},{2,3},{3,2},{4,5},{5,4},{6,7},{7,6},{8,9},{9,8},{10,11... | collective-permute-start | bytes 983048 | tf_op jit(solution)/shard_map/ppermute | solution.py:365
  2.7 0.7 %copy-start.4 = (s32[1,1,24]{2,1,0:T(1,128)S(1)}, s32[1,1,24]{2,1,0:T(1,128)}, u32[]{:S(2)}) copy-start(s32[1,1,24]{2,1,0:T(1,128)} %param.10) | copy-start | bytes 292
  2.7 0.7 %copy-start.5 = (s32[1,1,24]{2,1,0:T(1,128)S(1)}, s32[1,1,24]{2,1,0:T(1,128)}, u32[]{:S(2)}) copy-start(s32[1,1,24]{2,1,0:T(1,128)} %param.11) | copy-start | bytes 292
  3.3 1.0 %copy-start = (f32[1,5,4,16,256]{4,3,2,1,0:T(8,128)S(1)}, f32[1,5,4,16,256]{4,3,2,1,0:T(8,128)}, u32[]{:S(2)}) copy-start(f32[1,5,4,16,256]{4,3,2,1,0:T(8,128)} %param.6) | copy-start | bytes 983044
  4.3 1.0 %copy-start.1 = (f32[1,2,2,5,16,256]{5,4,3,2,1,0:T(8,128)S(1)}, f32[1,2,2,5,16,256]{5,4,3,2,1,0:T(8,128)}, u32[]{:S(2)}) copy-start(f32[1,2,2,5,16,256]{5,4,3,2,1,0:T(8,128)} %param.7) | copy-start | bytes 983044
  7.1 16.0 %copy-start.2 = (f32[1,1,24,5,128]{4,2,3,1,0:T(8,128)S(1)}, f32[1,1,24,5,128]{4,2,3,1,0:T(8,128)}, u32[]{:S(2)}) copy-start(f32[1,1,24,5,128]{4,2,3,1,0:T(8,128)} %param.8) | copy-start | bytes 184324
  7.1 16.0 %copy-start.3 = (f32[1,1,24,5,128]{4,2,3,1,0:T(8,128)S(1)}, f32[1,1,24,5,128]{4,2,3,1,0:T(8,128)}, u32[]{:S(2)}) copy-start(f32[1,1,24,5,128]{4,2,3,1,0:T(8,128)} %param.9) | copy-start | bytes 184324

commit v2 on v1

--- a/solution.py
+++ b/solution.py
@@ -129,6 +129,255 @@
         before, low_face = here, face
 
 
+def step_state(state, change, high_face, low_face):
+    half = 0.5 * time_step
+    return [
+        both(lambda u, c, h, l: u - half * (c + (h - l)), u, c, h, l)
+        for u, c, h, l in zip(state, change, high_face, low_face)
+    ]
+
+
+def split_z(ref, slot, field, half_across):
+    return tuple(
+        jnp.concatenate(
+            [
+                ref[slot, field, piece, pl.ds(parity, half_across, stride=2), :]
+                for piece in range(ref.shape[2])
+            ],
+            axis=1,
+        )
+        for parity in (0, 1)
+    )
+
+
+def put_layer(stage_ref, slot, new_ref, layer, state, turn):
+    fields, pieces, _, lanes = stage_ref.shape[1:]
+    half_across = state[0][0].shape[0]
+    for f in range(fields):
+        for piece in range(pieces):
+            part = slice(piece * lanes, (piece + 1) * lanes)
+            for parity in (0, 1):
+                values = state[f][parity][:, part]
+                stage_ref[slot, f, piece, pl.ds(parity, half_across, stride=2), :] = (
+                    turn * values if f == 1 else values
+                )
+            new_ref[f, layer, :, part] = stage_ref[slot, f, piece]
+
+
+class Carried:
+
+    def __init__(self, ref, slot, fields):
+        def pair(index):
+            return tuple(ref[slot, index, parity] for parity in (0, 1))
+
+        self.state = [pair(f) for f in range(fields)]
+        self.flux = [[self.state[1]] + [pair(fields + f) for f in range(1, fields)]]
+        self.speed = [pair(fields)]
+        self.partial = [pair(2 * fields + f) for f in range(fields)]
+
+    @staticmethod
+    def keep(ref, slot, cells, change, low_face):
+        half = 0.5 * time_step
+        fields = len(cells.state)
+        for f in range(fields):
+            for parity in (0, 1):
+                ref[slot, f, parity] = cells.state[f][parity]
+                ref[slot, 2 * fields + f, parity] = cells.state[f][parity] - half * (
+                    change[f][parity] - low_face[f][parity]
+                )
+                ref[slot, fields + f, parity] = (
+                    cells.flux[0][f][parity] if f > 0 else cells.speed[0][parity]
+                )
+
+    def finished(self, high_face):
+        half = 0.5 * time_step
+        return [both(lambda p, h: p - half * h, p, h) for p, h in zip(self.partial, high_face)]
+
+
+def early_kernel(
+    groups, capacity, fine_ref, ghost_ref, owner_ref, column_ref,
+    new_ref, carry_ref, face_ref, sum_ref, select_ref, code_ref,
+    stage_ref, owner_vmem, column_vmem, copy_sems,
+):
+    _, fields, along, across, depth = fine_ref.shape
+    half_across = across // 2
+    lanes = stage_ref.shape[-1]
+    pieces = depth // lanes
+    at_high = lax.axis_index("box") == 1
+    side = jnp.where(at_high, 1, 0)
+    turn = jnp.where(at_high, -1.0, 1.0)
+
+    copies = {}
+
+    def fetch(slot, source):
+        for piece in range(pieces):
+            copies[slot, piece] = pltpu.make_async_copy(
+                source(slice(piece * lanes, (piece + 1) * lanes)),
+                stage_ref.at[slot, :, piece],
+                copy_sems.at[slot * pieces + piece],
+            )
+            copies[slot, piece].start()
+
+    ghost_slots = (0, along + 1)
+    fetch(0, lambda part: ghost_ref.at[0, 0, side, :, :, part])
+    for index in range(along):
+        layer = jnp.where(at_high, along - 1 - index, index)
+        fetch(1 + index, lambda part, layer=layer: fine_ref.at[0, :, layer, :, part])
+    fetch(along + 1, lambda part: ghost_ref.at[0, 1, side, :, :, part])
+    small = [
+        pltpu.make_async_copy(owner_ref, owner_vmem, copy_sems.at[(along + 2) * pieces]),
+        pltpu.make_async_copy(column_ref, column_vmem, copy_sems.at[(along + 2) * pieces + 1]),
+    ]
+    for copy in small:
+        copy.start()
+
+    def arrived(slot):
+        for piece in range(pieces):
+            copies[slot, piece].wait()
+        planes = [split_z(stage_ref, slot, f, half_across) for f in range(fields)]
+        planes[1] = tuple(turn * values for values in planes[1])
+        return planes
+
+    ghost_now = arrived(0)
+    before, low_face, change = Cells(ghost_now), None, None
+    faces = []
+    halves = []
+    for index in range(along):
+        here = Cells(arrived(1 + index))
+        face = x_face(before, here)
+        if index == 0:
+            faces.append(face)
+        else:
+            halves.append(step_state(before.state, change, face, low_face))
+        change = side_change(here)
+        before, low_face = here, face
+    Carried.keep(carry_ref, 0, before, change, low_face)
+
+    ghost_end = arrived(along + 1)
+    before = Cells(
+        [both(lambda a, b: 0.5 * a + 0.5 * b, a, b) for a, b in zip(ghost_now, ghost_end)]
+    )
+    low_face, change = None, None
+    total_sums = {}
+    for index in range(along - 1):
+        here = Cells(halves[index])
+        face = x_face(before, here)
+        if index == 0:
+            faces.append(face)
+        else:
+            state = step_state(before.state, change, face, low_face)
+            layer = jnp.where(at_high, along - index, index - 1)
+            put_layer(stage_ref, along + 1 + index, new_ref, layer, state, turn)
+            for f in range(fields):
+                key = (index - 1) // 2, f
+                pooled = state[f][0] + state[f][1]
+                total_sums[key] = total_sums[key] + pooled if key in total_sums else pooled
+        change = side_change(here)
+        before, low_face = here, face
+    Carried.keep(carry_ref, 1, before, change, low_face)
+    for (plane, f), pooled in total_sums.items():
+        sum_ref[plane, f] = pooled
+    for f in range(fields):
+        both_steps = [faces[0][f][parity] + faces[1][f][parity] for parity in (0, 1)]
+        face_ref[f] = both_steps[0] + both_steps[1]
+
+    for copy in small:
+        copy.wait()
+    total = owner_vmem.shape[1]
+    count_average = (along // 2) * half_across
+    selections = one_hot_slots(owner_vmem[...], groups, capacity)
+    record_ids = lax.broadcasted_iota(jnp.int32, (1, total), 1)
+    codes = (column_vmem[...] + 1).astype(jnp.float32)
+    codes = jnp.where(record_ids < count_average, codes, -codes)
+    for slot in range(capacity):
+        rows = slice(slot * groups, (slot + 1) * groups)
+        select_ref[rows] = selections[slot]
+        code = jnp.sum(selections[slot] * codes, axis=1, keepdims=True)
+        code_ref[rows] = jnp.broadcast_to(code, (groups, code_ref.shape[1]))
+
+
+def late_kernel(
+    groups, capacity, rows, carry_ref, other_ref, face_ref, sum_ref, select_ref, code_ref,
+    early_ref, new_ref, out_ref, stage_ref,
+):
+    del early_ref
+    fields, along, across, depth = other_ref.shape
+    half_across = across // 2
+    lanes = stage_ref.shape[-1]
+    pieces = depth // lanes
+    at_high = lax.axis_index("box") == 1
+    turn = jnp.where(at_high, -1.0, 1.0)
+
+    def place(index):
+        return jnp.where(at_high, along - 1 - index, index)
+
+    def received(index):
+        for f in range(fields):
+            plane = other_ref[f, place(index)]
+            for piece in range(pieces):
+                stage_ref[index, f, piece] = plane[:, piece * lanes:(piece + 1) * lanes]
+        planes = [split_z(stage_ref, index, f, half_across) for f in range(fields)]
+        planes[1] = tuple(turn * values for values in planes[1])
+        return planes
+
+    near = Cells(received(0))
+    end = Carried(carry_ref, 0, fields)
+    end_face = x_face(end, near)
+    end_half = end.finished(end_face)
+    near_half = step_state(
+        near.state, side_change(near), x_face(near, Cells(received(1))), end_face
+    )
+    inner = Carried(carry_ref, 1, fields)
+    last = Cells(end_half)
+    inner_face = x_face(inner, last)
+    inner_new = inner.finished(inner_face)
+    last_new = step_state(
+        last.state, side_change(last), x_face(last, Cells(near_half)), inner_face
+    )
+    put_layer(stage_ref, 2, new_ref, place(along - 2), inner_new, turn)
+    put_layer(stage_ref, 3, new_ref, place(along - 1), last_new, turn)
+
+    planes = along // 2
+    blocks = []
+    for f in range(fields):
+        sums = [sum_ref[plane, f] for plane in range(planes - 1)]
+        sums.append(
+            (inner_new[f][0] + inner_new[f][1]) + (last_new[f][0] + last_new[f][1])
+        )
+        scale = turn if f == 1 else 1.0
+        for plane in range(planes):
+            blocks.append(
+                (0.125 * scale) * jnp.where(at_high, sums[planes - 1 - plane], sums[plane])
+            )
+        blocks.append((-0.5 * time_step / 8 * scale) * face_ref[f])
+    route(
+        jnp.concatenate(blocks, axis=0), select_ref[...], groups, capacity, rows, fields, out_ref
+    )
+    for slot in range(capacity):
+        out_ref[pl.ds(slot * (fields + 1) + fields, groups, stride=rows), :] = code_ref[
+            slot * groups:(slot + 1) * groups
+        ]
+
+
+def route(stacked, selection, groups, capacity, rows, fields, out_ref):
+    depth, coarse_depth = stacked.shape[1], out_ref.shape[1]
+    lane_pair = lax.broadcasted_iota(jnp.int32, (depth, coarse_depth), 0) // 2
+    pool = jnp.where(
+        lane_pair == lax.broadcasted_iota(jnp.int32, (depth, coarse_depth), 1), 1.0, 0.0
+    )
+    records = split_dot(stacked, pool, True)
+    total = records.shape[0] // fields
+    wide = jnp.concatenate(
+        [records[f * total:(f + 1) * total] for f in range(fields)], axis=1
+    )
+    chosen = split_dot(selection, wide, False)
+    for slot in range(capacity):
+        for f in range(fields):
+            out_ref[pl.ds(slot * (fields + 1) + f, groups, stride=rows), :] = chosen[
+                slot * groups:(slot + 1) * groups, f * coarse_depth:(f + 1) * coarse_depth
+            ]
+
+
 def one_hot_slots(owners, groups, capacity):
     total = owners.shape[1]
     hit = owners == lax.broadcasted_iota(jnp.int32, (groups, total), 0)
@@ -147,53 +396,29 @@
 
 def patch_kernel(
     box_count, groups, capacity, rows,
-    box_ref, fine_ref, ghost_ref, low_ref, high_ref, owner_ref, column_ref,
+    fine_ref, ghost_ref, low_ref, high_ref, owner_ref, column_ref,
     new_ref, out_ref, half_ref, stage_ref,
 ):
-    box_place = box_ref[0]
+    box_place = lax.axis_index("box")
     at_low = box_place == 0
     at_high = box_place == box_count - 1
     fields, along, across, depth = fine_ref.shape
     half_across = across // 2
     lanes = stage_ref.shape[-1]
     pieces = depth // lanes
-    mirrored = box_count == 2
-    side = jnp.where(at_high, 1, 0) if mirrored else 0
-    turn = jnp.where(at_high, -1.0, 1.0)
-
-    def place(index):
-        return jnp.where(at_high, along - 1 - index, index) if mirrored else index
-
-    def oriented(field, values):
-        return turn * values if mirrored and field == 1 else values
-
     slots = iter(range(stage_ref.shape[0]))
 
     def parted(planes):
         slot = next(slots)
         for f, plane in enumerate(planes):
             for piece in range(pieces):
-                stage_ref[slot, f, piece] = oriented(f, plane[:, piece * lanes:(piece + 1) * lanes])
-        return [
-            tuple(
-                jnp.concatenate(
-                    [
-                        stage_ref[slot, f, piece, pl.ds(parity, half_across, stride=2), :]
-                        for piece in range(pieces)
-                    ],
-                    axis=1,
-                )
-                for parity in (0, 1)
-            )
-            for f in range(fields)
-        ]
+                stage_ref[slot, f, piece] = plane[:, piece * lanes:(piece + 1) * lanes]
+        return [split_z(stage_ref, slot, f, half_across) for f in range(fields)]
 
     def rows_of(ref, layer):
         return parted([ref[f, layer] for f in range(fields)])
 
     def ghost_layer(at, time_frac):
-        if time_frac == 0.0:
-            return parted([ghost_ref[0, at, f] for f in range(fields)])
         return parted(
             [
                 (1.0 - time_frac) * ghost_ref[0, at, f] + time_frac * ghost_ref[1, at, f]
@@ -207,53 +432,26 @@
     def picked(flag, first, second):
         return [both(lambda a, b: jnp.where(flag, a, b), a, b) for a, b in zip(first, second)]
 
-    def fine_layer(index):
-        return rows_of(fine_ref, place(index))
-
-    inner = [functools.partial(fine_layer, index) for index in range(along)]
-    low_faces, high_faces = [], []
-    if mirrored:
-        start = 0
-        first = [lambda: ghost_layer(side, 0.0), *inner]
-        first += [lambda: rows_of(low_ref, place(0)), lambda: rows_of(low_ref, place(1))]
-        second = [lambda: ghost_layer(side, 0.5)]
-        second += [functools.partial(half_layer, index) for index in range(along + 1)]
-        low_at = (0, 0)
-        high_at = (-1, -1)
-    else:
-        start = 1
-        width = low_ref.shape[1]
-        first = [lambda: rows_of(low_ref, width - 2)]
-        first += [
-            lambda: picked(at_low, ghost_layer(0, 0.0), rows_of(low_ref, width - 1)),
-            *inner,
-            lambda: picked(at_high, ghost_layer(1, 0.0), rows_of(high_ref, 0)),
-            lambda: rows_of(high_ref, 1),
-        ]
-        second = [lambda: picked(at_low, ghost_layer(0, 0.5), half_layer(0))]
-        second += [functools.partial(half_layer, 1 + index) for index in range(along)]
-        second += [lambda: picked(at_high, ghost_layer(1, 0.5), half_layer(along + 1))]
-        low_at = (1, 0)
-        high_at = (along + 1, along)
+    width = low_ref.shape[1]
+    first = [lambda: rows_of(low_ref, width - 2)]
+    first += [lambda: picked(at_low, ghost_layer(0, 0.0), rows_of(low_ref, width - 1))]
+    first += [functools.partial(rows_of, fine_ref, index) for index in range(along)]
+    first += [lambda: picked(at_high, ghost_layer(1, 0.0), rows_of(high_ref, 0))]
+    first += [lambda: rows_of(high_ref, 1)]
+    second = [lambda: picked(at_low, ghost_layer(0, 0.5), half_layer(0))]
+    second += [functools.partial(half_layer, 1 + index) for index in range(along)]
+    second += [lambda: picked(at_high, ghost_layer(1, 0.5), half_layer(along + 1))]
+    low_at, high_at = (1, 0), (along + 1, along)
+    low_faces, high_faces, sums = [], [], {}
 
     def keep_half(index, state):
         for f in range(fields):
             for parity in (0, 1):
                 half_ref[index - 1, f, parity] = state[f][parity]
 
-    sums = {}
-
     def keep_new(index, state):
-        slot = next(slots)
-        layer = place(index - 1)
+        put_layer(stage_ref, next(slots), new_ref, index - 1, state, 1.0)
         for f in range(fields):
-            for piece in range(pieces):
-                part = slice(piece * lanes, (piece + 1) * lanes)
-                for parity in (0, 1):
-                    stage_ref[slot, f, piece, pl.ds(parity, half_across, stride=2), :] = oriented(
-                        f, state[f][parity][:, part]
-                    )
-                new_ref[f, layer, :, part] = stage_ref[slot, f, piece]
             pooled = state[f][0] + state[f][1]
             key = (f, (index - 1) // 2)
             sums[key] = sums[key] + pooled if key in sums else pooled
@@ -272,50 +470,34 @@
     planes = along // 2
     blocks = []
     for f in range(fields):
-        for plane in range(planes):
-            if mirrored:
-                value = jnp.where(at_high, sums[f, planes - 1 - plane], sums[f, plane])
-            else:
-                value = sums[f, plane]
-            blocks.append(oriented(f, 0.125 * value))
-        low = [sum(halves) for halves in zip(*(step[f] for step in low_faces))]
-        face_sum = low[0] + low[1]
-        if not mirrored:
-            high = [sum(halves) for halves in zip(*(step[f] for step in high_faces))]
-            face_sum = jnp.where(at_low, face_sum, -(high[0] + high[1]))
-        blocks.append(oriented(f, (-0.5 * time_step / 8) * face_sum))
-    stacked = jnp.concatenate(blocks, axis=0)
-    coarse_depth = depth // 2
-    lane_pair = lax.broadcasted_iota(jnp.int32, (depth, coarse_depth), 0) // 2
-    pool = jnp.where(
-        lane_pair == lax.broadcasted_iota(jnp.int32, (depth, coarse_depth), 1), 1.0, 0.0
-    )
-    records = split_dot(stacked, pool, True)
-
+        blocks += [0.125 * sums[f, plane] for plane in range(planes)]
+        low = [low_faces[0][f][parity] + low_faces[1][f][parity] for parity in (0, 1)]
+        high = [high_faces[0][f][parity] + high_faces[1][f][parity] for parity in (0, 1)]
+        face_sum = jnp.where(at_low, low[0] + low[1], -(high[0] + high[1]))
+        blocks.append((-0.5 * time_step / 8) * face_sum)
     total = owner_ref.shape[1]
-    count_average = planes * half_across
     selections = one_hot_slots(owner_ref[...], groups, capacity)
-    wide = jnp.concatenate(
-        [records[f * total:(f + 1) * total] for f in range(fields)], axis=1
-    )
-    chosen = split_dot(jnp.concatenate(selections, axis=0), wide, False)
+    route(
+        jnp.concatenate(blocks, axis=0), jnp.concatenate(selections, axis=0),
+        groups, capacity, rows, fields, out_ref,
+    )
     record_ids = lax.broadcasted_iota(jnp.int32, (1, total), 1)
     codes = (column_ref[...] + 1).astype(jnp.float32)
-    face_code = -codes if mirrored else jnp.where(at_low | at_high, -codes, 0.0)
-    codes = jnp.where(record_ids < count_average, codes, face_code)
+    face_code = jnp.where(at_low | at_high, -codes, 0.0)
+    codes = jnp.where(record_ids < planes * half_across, codes, face_code)
     for slot in range(capacity):
-        base = slot * (fields + 1)
-        for f in range(fields):
-            out_ref[pl.ds(base + f, groups, stride=rows), :] = chosen[
-                slot * groups:(slot + 1) * groups, f * coarse_depth:(f + 1) * coarse_depth
-            ]
         code = jnp.sum(selections[slot] * codes, axis=1, keepdims=True)
-        out_ref[pl.ds(base + fields, groups, stride=rows), :] = jnp.broadcast_to(
-            code, (groups, coarse_depth)
+        out_ref[pl.ds(slot * (fields + 1) + fields, groups, stride=rows), :] = jnp.broadcast_to(
+            code, (groups, out_ref.shape[1])
         )
 
 
-def owner_kernel(groups, capacity, rows, in_ref, state_ref, term_ref, out_ref):
+def owner_kernel(
+    groups, capacity, rows, in_ref, state_ref, term_ref, new_ref,
+    coarse_ref, final_ref, out_ref, copy_sems,
+):
+    write_fine = pltpu.make_async_copy(new_ref, final_ref, copy_sems.at[0])
+    write_fine.start()
     fields, total, coarse_depth = state_ref.shape
     codes, values = [], []
     for slot in range(capacity):
@@ -347,12 +529,15 @@
         state = state_ref[f]
         refluxed = state + (value - term_ref[f])
         out_ref[f] = jnp.where(flag > 0.0, value, jnp.where(flag < 0.0, refluxed, state))
+    write_coarse = pltpu.make_async_copy(out_ref, coarse_ref, copy_sems.at[1])
+    write_coarse.start()
+    write_fine.wait()
+    write_coarse.wait()
 
 
 def on_device(fine_state, patch_ghosts, coarse_state, coarse_face_term, dest_grp, dest_column):
     box_count = lax.axis_size("box")
     group_count = lax.axis_size("grp")
-    box_place = lax.axis_index("box")
     current = fine_state[0]
     fields, cells_along, cells_across, cells_depth = current.shape
     total = dest_grp.shape[-1]
@@ -360,54 +545,99 @@
     rows = -(-capacity * (fields + 1) // 8) * 8
     coarse_depth = cells_depth // 2
     params = pltpu.CompilerParams(vmem_limit_bytes=vmem_limit)
+    vmem = pl.BlockSpec(memory_space=pltpu.VMEM)
+    hbm = pl.BlockSpec(memory_space=pltpu.HBM)
+    half_across, pieces = cells_across // 2, cells_depth // 128
+    outgoing_shape = jax.ShapeDtypeStruct((group_count * rows, coarse_depth), jnp.float32)
+
+    def stage(count):
+        return pltpu.VMEM((count, fields, pieces, cells_across, 128), jnp.float32)
 
     if box_count == 2:
-        low = lax.ppermute(current, "box", [(0, 1), (1, 0)])
-        high = low
+        other = lax.ppermute(current, "box", [(0, 1), (1, 0)])
+        copies = (cells_along + 2) * pieces + 2
+        shapes = [
+            current.shape,
+            (2, 3 * fields, 2, half_across, cells_depth),
+            (fields, half_across, cells_depth),
+            (cells_along // 2 - 1, fields, half_across, cells_depth),
+            (capacity * group_count, total),
+            (capacity * group_count, coarse_depth),
+        ]
+        early, carry, face, sums, selection, codes = pl.pallas_call(
+            functools.partial(early_kernel, group_count, capacity),
+            out_shape=[pltpu.VMEM(shape, jnp.float32) for shape in shapes],
+            in_specs=[hbm] * 4,
+            out_specs=[vmem] * len(shapes),
+            scratch_shapes=[
+                stage(2 * cells_along),
+                pltpu.VMEM((1, total), jnp.int32),
+                pltpu.VMEM((1, total), jnp.int32),
+                pltpu.SemaphoreType.DMA((copies,)),
+            ],
+            compiler_params=params,
+            cost_estimate=pl.CostEstimate(
+                flops=200 * current.size, bytes_accessed=8 * current.size, transcendentals=0
+            ),
+            name="early",
+        )(*(
+            pltpu.with_memory_space_constraint(values, pltpu.HBM)
+            for values in (fine_state, patch_ghosts, dest_grp[0], dest_column[0])
+        ))
+        updated, outgoing = pl.pallas_call(
+            functools.partial(late_kernel, group_count, capacity, rows),
+            out_shape=[
+                pltpu.VMEM(current.shape, jnp.float32),
+                pltpu.VMEM(outgoing_shape.shape, jnp.float32),
+            ],
+            in_specs=[vmem] * 7,
+            out_specs=[vmem] * 2,
+            scratch_shapes=[stage(4)],
+            input_output_aliases={6: 0},
+            compiler_params=params,
+            name="late",
+        )(carry, other, face, sums, selection, codes, early)
     else:
         ends = box_count - 1
         low = lax.ppermute(current[:, -2:], "box", [(i, i + 1) for i in range(ends)])
         high = lax.ppermute(current[:, :2], "box", [(i + 1, i) for i in range(ends)])
-
-    vmem = pl.BlockSpec(memory_space=pltpu.VMEM)
-    halves = cells_along + (1 if box_count == 2 else 2)
-    updated, outgoing = pl.pallas_call(
-        functools.partial(patch_kernel, box_count, group_count, capacity, rows),
-        out_shape=(
-            jax.ShapeDtypeStruct(current.shape, jnp.float32),
-            jax.ShapeDtypeStruct((group_count * rows, coarse_depth), jnp.float32),
-        ),
-        in_specs=[pl.BlockSpec(memory_space=pltpu.SMEM)] + [vmem] * 6,
-        out_specs=(vmem, vmem),
-        scratch_shapes=[
-            pltpu.VMEM((halves, fields, 2, cells_across // 2, cells_depth), jnp.float32),
-            pltpu.VMEM(
-                (2 * cells_along + 8, fields, cells_depth // 128, cells_across, 128), jnp.float32
-            ),
-        ],
-        compiler_params=params,
-        name="patch",
-    )(
-        box_place.reshape(1), current, patch_ghosts[0], low, high,
-        dest_grp[0], dest_column[0],
-    )
+        updated, outgoing = pl.pallas_call(
+            functools.partial(patch_kernel, box_count, group_count, capacity, rows),
+            out_shape=[jax.ShapeDtypeStruct(current.shape, jnp.float32), outgoing_shape],
+            in_specs=[vmem] * 6,
+            out_specs=[vmem] * 2,
+            scratch_shapes=[
+                pltpu.VMEM((cells_along + 2, fields, 2, half_across, cells_depth), jnp.float32),
+                stage(2 * cells_along + 8),
+            ],
+            compiler_params=params,
+            name="patch",
+        )(current, patch_ghosts[0], low, high, dest_grp[0], dest_column[0])
     incoming = lax.all_to_all(
         outgoing.reshape(group_count, rows, coarse_depth),
         "grp", split_axis=0, concat_axis=0, tiled=True,
     ).reshape(group_count * rows, coarse_depth)
-    coarse_new = pl.pallas_call(
+    coarse_new, final = pl.pallas_call(
         functools.partial(owner_kernel, group_count, capacity, rows),
-        out_shape=jax.ShapeDtypeStruct((fields, total, coarse_depth), jnp.float32),
-        in_specs=[vmem] * 3,
-        out_specs=vmem,
+        out_shape=[
+            jax.ShapeDtypeStruct((fields, total, coarse_depth), jnp.float32),
+            jax.ShapeDtypeStruct(current.shape, jnp.float32),
+        ],
+        in_specs=[vmem] * 4,
+        out_specs=[hbm, hbm],
+        scratch_shapes=[
+            pltpu.VMEM((fields, total, coarse_depth), jnp.float32),
+            pltpu.SemaphoreType.DMA((2,)),
+        ],
         compiler_params=params,
         name="owner",
     )(
         incoming,
         coarse_state[0, 0].transpose(1, 0, 2),
         coarse_face_term[0, 0].transpose(1, 0, 2),
-    )
-    return (updated[None], coarse_new.transpose(1, 0, 2)[None, None])
+        pltpu.with_memory_space_constraint(updated, pltpu.VMEM),
+    )
+    return (final[None], coarse_new.transpose(1, 0, 2)[None, None])
 
 
 def solution(mesh):

time: 24.2 us -> 21.4 us (0.88)
  local copies, waits for them, and re-layouts: 2.62 us -> 0.01 us
  waiting for transfers between devices: 1.47 us -> 0.01 us
  Pallas kernels: 2.73 us -> 3.98 us
    unnamed x12 -> x4, local copies, waits for them, and re-layouts: 2.62 us -> 0.01 us
    ppermute x1, waiting for transfers between devices: 1.47 us -> 0.01 us  [on_device(): other = lax.ppermute(current, 'box', [(0, 1), (1, 0)])]
    pallas_call x1 -> x2, Pallas kernels: 1.87 us -> 3.1 us  [the longest x1 2.4 us: on_device(): pl.pallas_call(functools.partial(early_kernel, group_count, capacity), ou...]
  transfers between devices with their start and end apart: 1 -> 1, of which waited for: 1 -> 0; matrix products, arithmetic and copies ran while one was open for 0% -> 0% of each run, Pallas kernels for 0% -> 11%
where the time goes in v2:
time: 21.4 us; the launch traced here: 21.1 us
  blocking collectives  15.9 us (74%)
  Pallas kernels  3.98 us (19%)
  between operations  0.67 us (3%)
  starting transfers between devices  0.56 us (3%)
    all_to_all x1, blocking collectives, on_device(): lax.all_to_all(outgoing.reshape(group_count, rows, coarse_depth), 'grp',...  15.9 us
    pallas_call x1, Pallas kernels, on_device(): pl.pallas_call(functools.partial(early_kernel, group_count, capacity), ou...  2.4 us
    pallas_call x1, Pallas kernels, on_device(): pl.pallas_call(functools.partial(owner_kernel, group_count, capacity, row...  0.88 us
    pallas_call x1, Pallas kernels, on_device(): pl.pallas_call(functools.partial(late_kernel, group_count, capacity, rows...  0.7 us
    ppermute x1, starting transfers between devices, on_device(): other = lax.ppermute(current, 'box', [(0, 1), (1, 0)])  0.56 us
  transfers between devices with their start and end apart: 1, of which 0 were waited for; matrix products, arithmetic and copies ran while one was open for 0% of the time, Pallas kernels for 11%

profile of v2, /device:TPU:0, one launch (start us, length us, event | category | flops | bytes accessed | tf_op | source)
XLA Modules:
  0.0 21.1 jit_solution(8533768461477051038)
XLA Ops:
  0.6 0.6 %collective-permute-start = (f32[5,4,16,256]{3,2,1,0:T(8,128)}, f32[5,4,16,256]{3,2,1,0:T(8,128)S(1)}, u32[]{:S(2)}, u32[]{:S(2)}) collective-permute-start(f32[5,4,16,256]{3,2,1,0:T(8,128)} %bitcast.19), channel_id=1, source_target_pairs={{0,1},{1,0},{2,3},{3,2},{4,5},{5,4},{6,7},{7,6},{8,9},{9,8},{10,11... | collective-permute-start | bytes 983048 | tf_op jit(solution)/shard_map/ppermute | solution.py:557
  1.2 2.4 %early.1 = (f32[5,4,16,256]{3,2,1,0:T(8,128)S(1)}, f32[2,15,2,8,256]{4,3,2,1,0:T(8,128)S(1)}, f32[5,8,256]{2,1,0:T(8,128)S(1)}, f32[1,5,8,256]{3,2,1,0:T(8,128)S...) custom-call(f32[1,5,4,16,256]{4,3,2,1,0:T(8,128)} %fine_ref.1, f32[1,2,2,5,16,256]{5,4,3,2,1,0:T(8,128)} %ghost_ref.1, ...), custom_call_target="tpu_custom_call" | custom-call | flops 16384000 | bytes 655360 | tf_op jit(solution)/shard_map/early/pallas_call | solution.py:567
  3.6 0.0 collective-permute-done.other_ref
  3.6 0.7 %late.1 = (f32[5,4,16,256]{3,2,1,0:T(8,128)S(1)}, f32[256,128]{1,0:T(8,128)S(1)}) custom-call(f32[2,15,2,8,256]{4,3,2,1,0:T(8,128)S(1)} %get-tuple-element.12.carry_ref, f32[5,4,16,256]{3,2,1,0:T(8,128)S(1)} %collective-permute-done.other_ref, f32[5,8,256]{2,1,0:T(8,128)S(1)} %get-tuple-element.13.face_ref, ...), custom_call_target="tpu_custom_call", output_to_operand_aliasing={{0}: (6, {})} | custom-call | tf_op jit(solution)/shard_map/late/pallas_call | solution.py:587
  4.3 0.0 copy-start
  4.3 0.0 copy-start.1
  4.3 15.9 %all_to_all.5 = f32[16,16,128]{2,1,0:T(8,128)S(1)} all-to-all(f32[16,16,128]{2,1,0:T(8,128)S(1)} %bitcast.16), channel_id=1, replica_groups=mesh['grp'=16,'box'=2] {'grp'}, dimensions={0} | all-to-all | bytes 262144 | tf_op jit(solution)/shard_map/all_to_all | solution.py:616
  20.2 0.0 copy-done
  20.2 0.0 copy-done.1
  20.2 0.9 %owner.1 = (f32[5,24,128]{2,1,0:T(8,128)}, f32[5,4,16,256]{3,2,1,0:T(8,128)}) custom-call(f32[256,128]{1,0:T(8,128)S(1)} %bitcast.15, f32[5,24,128]{2,1,0:T(8,128)S(1)} %bitcast.17, f32[5,24,128]{2,1,0:T(8,128)S(1)} %bitcast.18, f32[5,4,16,256]{3,2,1,0:T(8,128)S(1)} %get-tuple-element.19.new_ref), custom_call_target="tpu_custom_call" | custom-call | tf_op jit(solution)/shard_map/owner/pallas_call | solution.py:620
Async XLA Ops:
  0.6 3.0 %collective-permute-start = (f32[5,4,16,256]{3,2,1,0:T(8,128)}, f32[5,4,16,256]{3,2,1,0:T(8,128)S(1)}, u32[]{:S(2)}, u32[]{:S(2)}) collective-permute-start(f32[5,4,16,256]{3,2,1,0:T(8,128)} %bitcast.19), channel_id=1, source_target_pairs={{0,1},{1,0},{2,3},{3,2},{4,5},{5,4},{6,7},{7,6},{8,9},{9,8},{10,11... | collective-permute-start | bytes 983048 | tf_op jit(solution)/shard_map/ppermute | solution.py:557
  4.3 15.9 %copy-start = (f32[1,1,24,5,128]{4,2,3,1,0:T(8,128)S(1)}, f32[1,1,24,5,128]{4,2,3,1,0:T(8,128)}, u32[]{:S(2)}) copy-start(f32[1,1,24,5,128]{4,2,3,1,0:T(8,128)} %param.8) | copy-start | bytes 184324
  4.3 15.9 %copy-start.1 = (f32[1,1,24,5,128]{4,2,3,1,0:T(8,128)S(1)}, f32[1,1,24,5,128]{4,2,3,1,0:T(8,128)}, u32[]{:S(2)}) copy-start(f32[1,1,24,5,128]{4,2,3,1,0:T(8,128)} %param.9) | copy-start | bytes 184324

commit v3 on v2

--- a/solution.py
+++ b/solution.py
@@ -1,4 +1,5 @@
 import functools
+import math
 
 import jax
 import jax.numpy as jnp
@@ -61,7 +62,8 @@
             lambda e, a, b, c: (gamma_ratio - 1.0) * (e - 0.5 * (a + b + c)),
             state[4], square[0, 0], square[1, 1], square[2, 2],
         )
-        sound = both(lambda p, r: jnp.sqrt(gamma_ratio * p * r), pressure, inverse)
+        square_sound = both(lambda p, r: gamma_ratio * p * r, pressure, inverse)
+        sound = both(lambda q: q * lax.rsqrt(q), square_sound)
         enthalpy = both(jnp.add, state[4], pressure)
         self.state = state
         self.flux = []
@@ -195,8 +197,8 @@
 
 
 def early_kernel(
-    groups, capacity, fine_ref, ghost_ref, owner_ref, column_ref,
-    new_ref, carry_ref, face_ref, sum_ref, select_ref, code_ref,
+    groups, capacity, fine_ref, ghost_ref, owner_ref, column_ref, state_ref, term_ref,
+    new_ref, carry_ref, face_ref, sum_ref, select_ref, code_ref, state_vmem, term_vmem,
     stage_ref, owner_vmem, column_vmem, copy_sems,
 ):
     _, fields, along, across, depth = fine_ref.shape
@@ -224,16 +226,22 @@
         layer = jnp.where(at_high, along - 1 - index, index)
         fetch(1 + index, lambda part, layer=layer: fine_ref.at[0, :, layer, :, part])
     fetch(along + 1, lambda part: ghost_ref.at[0, 1, side, :, :, part])
+    pairs = (
+        (owner_ref, owner_vmem), (column_ref, column_vmem),
+        (state_ref, state_vmem), (term_ref, term_vmem),
+    )
     small = [
-        pltpu.make_async_copy(owner_ref, owner_vmem, copy_sems.at[(along + 2) * pieces]),
-        pltpu.make_async_copy(column_ref, column_vmem, copy_sems.at[(along + 2) * pieces + 1]),
+        pltpu.make_async_copy(source, target, copy_sems.at[(along + 2) * pieces + index])
+        for index, (source, target) in enumerate(pairs)
     ]
     for copy in small:
         copy.start()
 
     def arrived(slot):
-        for piece in range(pieces):
-            copies[slot, piece].wait()
+        if slot in (0, 3):
+            for (at, _), copy in copies.items():
+                if (at < 3) == (slot == 0):
+                    copy.wait()
         planes = [split_z(stage_ref, slot, f, half_across) for f in range(fields)]
         planes[1] = tuple(turn * values for values in planes[1])
         return planes
@@ -542,8 +550,11 @@
     fields, cells_along, cells_across, cells_depth = current.shape
     total = dest_grp.shape[-1]
     capacity = (total + group_count - 1) // group_count
-    rows = -(-capacity * (fields + 1) // 8) * 8
+    rows = capacity * (fields + 1)
+    inner_rows = math.gcd(rows, 8)
     coarse_depth = cells_depth // 2
+    owned_state = coarse_state[0, 0].transpose(1, 0, 2)
+    owned_term = coarse_face_term[0, 0].transpose(1, 0, 2)
     params = pltpu.CompilerParams(vmem_limit_bytes=vmem_limit)
     vmem = pl.BlockSpec(memory_space=pltpu.VMEM)
     hbm = pl.BlockSpec(memory_space=pltpu.HBM)
@@ -555,7 +566,7 @@
 
     if box_count == 2:
         other = lax.ppermute(current, "box", [(0, 1), (1, 0)])
-        copies = (cells_along + 2) * pieces + 2
+        copies = (cells_along + 2) * pieces + 4
         shapes = [
             current.shape,
             (2, 3 * fields, 2, half_across, cells_depth),
@@ -563,11 +574,13 @@
             (cells_along // 2 - 1, fields, half_across, cells_depth),
             (capacity * group_count, total),
             (capacity * group_count, coarse_depth),
+            owned_state.shape,
+            owned_term.shape,
         ]
-        early, carry, face, sums, selection, codes = pl.pallas_call(
+        early, carry, face, sums, selection, codes, owned_state, owned_term = pl.pallas_call(
             functools.partial(early_kernel, group_count, capacity),
             out_shape=[pltpu.VMEM(shape, jnp.float32) for shape in shapes],
-            in_specs=[hbm] * 4,
+            in_specs=[hbm] * 6,
             out_specs=[vmem] * len(shapes),
             scratch_shapes=[
                 stage(2 * cells_along),
@@ -582,7 +595,9 @@
             name="early",
         )(*(
             pltpu.with_memory_space_constraint(values, pltpu.HBM)
-            for values in (fine_state, patch_ghosts, dest_grp[0], dest_column[0])
+            for values in (
+                fine_state, patch_ghosts, dest_grp[0], dest_column[0], owned_state, owned_term
+            )
         ))
         updated, outgoing = pl.pallas_call(
             functools.partial(late_kernel, group_count, capacity, rows),
@@ -614,7 +629,7 @@
             name="patch",
         )(current, patch_ghosts[0], low, high, dest_grp[0], dest_column[0])
     incoming = lax.all_to_all(
-        outgoing.reshape(group_count, rows, coarse_depth),
+        outgoing.reshape(group_count, rows // inner_rows, inner_rows, coarse_depth),
         "grp", split_axis=0, concat_axis=0, tiled=True,
     ).reshape(group_count * rows, coarse_depth)
     coarse_new, final = pl.pallas_call(
@@ -633,8 +648,8 @@
         name="owner",
     )(
         incoming,
-        coarse_state[0, 0].transpose(1, 0, 2),
-        coarse_face_term[0, 0].transpose(1, 0, 2),
+        pltpu.with_memory_space_constraint(owned_state, pltpu.VMEM),
+        pltpu.with_memory_space_constraint(owned_term, pltpu.VMEM),
         pltpu.with_memory_space_constraint(updated, pltpu.VMEM),
     )
     return (final[None], coarse_new.transpose(1, 0, 2)[None, None])

time: 21.4 us -> 20.5 us (0.958)
  blocking collectives: 15.9 us -> 15.4 us
  Pallas kernels: 3.98 us -> 3.75 us
    all_to_all x1, blocking collectives: 15.9 us -> 15.4 us  [on_device(): lax.all_to_all(outgoing.reshape(group_count, rows // inner_rows, inner_ro...]
where the time goes in v3:
time: 20.5 us; the launch traced here: 20.3 us
  blocking collectives  15.4 us (75%)
  Pallas kernels  3.75 us (18%)
  between operations  0.66 us (3%)
  starting transfers between devices  0.56 us (3%)
    all_to_all x1, blocking collectives, on_device(): lax.all_to_all(outgoing.reshape(group_count, rows // inner_rows, inner_ro...  15.4 us
    pallas_call x1, Pallas kernels, on_device(): pl.pallas_call(functools.partial(early_kernel, group_count, capacity), ou...  2.19 us
    pallas_call x1, Pallas kernels, on_device(): pl.pallas_call(functools.partial(owner_kernel, group_count, capacity, row...  0.88 us
    pallas_call x1, Pallas kernels, on_device(): pl.pallas_call(functools.partial(late_kernel, group_count, capacity, rows...  0.68 us
    ppermute x1, starting transfers between devices, on_device(): other = lax.ppermute(current, 'box', [(0, 1), (1, 0)])  0.56 us
  transfers between devices with their start and end apart: 1, of which 0 were waited for; matrix products, arithmetic and copies ran while one was open for 0% of the time, Pallas kernels for 11%

profile of v3, /device:TPU:0, one launch (start us, length us, event | category | flops | bytes accessed | tf_op | source)
XLA Modules:
  0.0 20.3 jit_solution(9942960974977186326)
XLA Ops:
  0.6 0.6 %collective-permute-start = (f32[5,4,16,256]{3,2,1,0:T(8,128)}, f32[5,4,16,256]{3,2,1,0:T(8,128)S(1)}, u32[]{:S(2)}, u32[]{:S(2)}) collective-permute-start(f32[5,4,16,256]{3,2,1,0:T(8,128)} %bitcast.17), channel_id=1, source_target_pairs={{0,1},{1,0},{2,3},{3,2},{4,5},{5,4},{6,7},{7,6},{8,9},{9,8},{10,11... | collective-permute-start | bytes 983048 | tf_op jit(solution)/shard_map/ppermute | solution.py:568
  1.2 2.2 %early.1 = (f32[5,4,16,256]{3,2,1,0:T(8,128)S(1)}, f32[2,15,2,8,256]{4,3,2,1,0:T(8,128)S(1)}, f32[5,8,256]{2,1,0:T(8,128)S(1)}, f32[1,5,8,256]{3,2,1,0:T(8,128)S...) custom-call(f32[1,5,4,16,256]{4,3,2,1,0:T(8,128)} %fine_ref.1, ...), custom_call_target="tpu_custom_call" | custom-call | flops 16384000 | bytes 655360 | tf_op jit(solution)/shard_map/early/pallas_call | solution.py:580
  3.4 0.0 collective-permute-done.other_ref
  3.4 0.7 %late.1 = (f32[5,4,16,256]{3,2,1,0:T(8,128)S(1)}, f32[192,128]{1,0:T(8,128)S(1)}) custom-call(f32[2,15,2,8,256]{4,3,2,1,0:T(8,128)S(1)} %get-tuple-element.14.carry_ref, f32[5,4,16,256]{3,2,1,0:T(8,128)S(1)} %collective-permute-done.other_ref, f32[5,8,256]{2,1,0:T(8,128)S(1)} %get-tuple-element.15.face_ref, ...), custom_call_target="tpu_custom_call", output_to_operand_aliasing={{0}: (6, {})} | custom-call | tf_op jit(solution)/shard_map/late/pallas_call | solution.py:602
  4.1 15.4 %all_to_all.5 = f32[16,3,4,128]{3,2,1,0:T(4,128)S(1)} all-to-all(f32[16,3,4,128]{3,2,1,0:T(4,128)S(1)} %bitcast.16), channel_id=1, replica_groups=mesh['grp'=16,'box'=2] {'grp'}, dimensions={0} | all-to-all | bytes 196608 | tf_op jit(solution)/shard_map/all_to_all | solution.py:631
  19.5 0.9 %owner.1 = (f32[5,24,128]{2,1,0:T(8,128)}, f32[5,4,16,256]{3,2,1,0:T(8,128)}) custom-call(f32[192,128]{1,0:T(8,128)S(1)} %bitcast.15, f32[5,24,128]{2,1,0:T(8,128)S(1)} %get-tuple-element.21.state_ref, f32[5,24,128]{2,1,0:T(8,128)S(1)} %get-tuple-element.22.term_ref, f32[5,4,16,256]{3,2,1,0:T(8,128)S(1)} %get-tuple-element.23.new_ref), custom_call_target="tpu_custom_call" | custom-call | tf_op jit(solution)/shard_map/owner/pallas_call | solution.py:635
Async XLA Ops:
  0.6 2.8 %collective-permute-start = (f32[5,4,16,256]{3,2,1,0:T(8,128)}, f32[5,4,16,256]{3,2,1,0:T(8,128)S(1)}, u32[]{:S(2)}, u32[]{:S(2)}) collective-permute-start(f32[5,4,16,256]{3,2,1,0:T(8,128)} %bitcast.17), channel_id=1, source_target_pairs={{0,1},{1,0},{2,3},{3,2},{4,5},{5,4},{6,7},{7,6},{8,9},{9,8},{10,11... | collective-permute-start | bytes 983048 | tf_op jit(solution)/shard_map/ppermute | solution.py:568

commit v4 on v3

--- a/solution.py
+++ b/solution.py
@@ -283,11 +283,19 @@
         change = side_change(here)
         before, low_face = here, face
     Carried.keep(carry_ref, 1, before, change, low_face)
-    for (plane, f), pooled in total_sums.items():
-        sum_ref[plane, f] = pooled
+    keys = sorted(total_sums)
+    blocks = [0.125 * total_sums[key] for key in keys]
     for f in range(fields):
         both_steps = [faces[0][f][parity] + faces[1][f][parity] for parity in (0, 1)]
-        face_ref[f] = both_steps[0] + both_steps[1]
+        blocks.append((-0.5 * time_step / 8) * (both_steps[0] + both_steps[1]))
+    records = pool_z(jnp.concatenate(blocks, axis=0), face_ref.shape[2])
+    for index, (plane, f) in enumerate([*keys, *((None, f) for f in range(fields))]):
+        record = records[index * half_across:(index + 1) * half_across]
+        record = turn * record if f == 1 else record
+        if plane is None:
+            face_ref[f] = record
+        else:
+            sum_ref[plane, f] = record
 
     for copy in small:
         copy.wait()
@@ -299,7 +307,9 @@
     codes = jnp.where(record_ids < count_average, codes, -codes)
     for slot in range(capacity):
         rows = slice(slot * groups, (slot + 1) * groups)
-        select_ref[rows] = selections[slot]
+        ids = record_ids.astype(jnp.float32)
+        record = jnp.sum(selections[slot] * ids, axis=1, keepdims=True)
+        select_ref[rows] = jnp.broadcast_to(record, (groups, code_ref.shape[1])).astype(jnp.int32)
         code = jnp.sum(selections[slot] * codes, axis=1, keepdims=True)
         code_ref[rows] = jnp.broadcast_to(code, (groups, code_ref.shape[1]))
 
@@ -346,34 +356,75 @@
     put_layer(stage_ref, 3, new_ref, place(along - 1), last_new, turn)
 
     planes = along // 2
-    blocks = []
+    records = []
     for f in range(fields):
+        scale = turn if f == 1 else 1.0
+        last_sum = (inner_new[f][0] + inner_new[f][1]) + (last_new[f][0] + last_new[f][1])
         sums = [sum_ref[plane, f] for plane in range(planes - 1)]
-        sums.append(
-            (inner_new[f][0] + inner_new[f][1]) + (last_new[f][0] + last_new[f][1])
+        sums.append((0.125 * scale) * pooled_z(last_sum))
+        records.append(
+            [jnp.where(at_high, sums[planes - 1 - plane], sums[plane]) for plane in range(planes)]
         )
-        scale = turn if f == 1 else 1.0
-        for plane in range(planes):
-            blocks.append(
-                (0.125 * scale) * jnp.where(at_high, sums[planes - 1 - plane], sums[plane])
-            )
-        blocks.append((-0.5 * time_step / 8 * scale) * face_ref[f])
-    route(
-        jnp.concatenate(blocks, axis=0), select_ref[...], groups, capacity, rows, fields, out_ref
-    )
+        records[f].append(face_ref[f])
+    if half_across == 8 and groups % 8 == 0:
+        place_rows(records, select_ref, groups, capacity, rows, out_ref)
+    else:
+        joined = jnp.concatenate([block for blocks in records for block in blocks], axis=0)
+        total = joined.shape[0] // fields
+        record_ids = lax.broadcasted_iota(jnp.int32, (capacity * groups, total), 1)
+        chosen = jnp.where(select_ref[:, :1] == record_ids, 1.0, 0.0)
+        route(joined, chosen, groups, capacity, rows, fields, out_ref)
     for slot in range(capacity):
         out_ref[pl.ds(slot * (fields + 1) + fields, groups, stride=rows), :] = code_ref[
             slot * groups:(slot + 1) * groups
         ]
 
 
-def route(stacked, selection, groups, capacity, rows, fields, out_ref):
-    depth, coarse_depth = stacked.shape[1], out_ref.shape[1]
+def pool_z(stacked, coarse_depth):
+    depth = stacked.shape[1]
     lane_pair = lax.broadcasted_iota(jnp.int32, (depth, coarse_depth), 0) // 2
     pool = jnp.where(
         lane_pair == lax.broadcasted_iota(jnp.int32, (depth, coarse_depth), 1), 1.0, 0.0
     )
-    records = split_dot(stacked, pool, True)
+    return split_dot(stacked, pool, True)
+
+
+def pooled_z(values):
+    lanes = 128
+    at = lax.broadcasted_iota(jnp.int32, (values.shape[0], lanes), 1)
+    even = (at * 2) & (lanes - 1)
+
+    def pairs(start):
+        block = values[:, start:start + lanes]
+        return jnp.take_along_axis(
+            block, even, axis=1, mode="promise_in_bounds"
+        ) + jnp.take_along_axis(block, even + 1, axis=1, mode="promise_in_bounds")
+
+    joined = [
+        jnp.where(at < lanes // 2, pairs(start), pairs(start + lanes))
+        for start in range(0, values.shape[1], 2 * lanes)
+    ]
+    return joined[0] if len(joined) == 1 else jnp.concatenate(joined, axis=1)
+
+
+def place_rows(records, select_ref, groups, capacity, rows, out_ref):
+    fields = len(records)
+    for slot in range(capacity):
+        for first in range(0, groups, 8):
+            at = slot * groups + first
+            chosen = select_ref[at:at + 8]
+            row = chosen & 7
+            for f in range(fields):
+                value = None
+                for plane, record in enumerate(records[f]):
+                    got = jnp.take_along_axis(record, row, axis=0, mode="promise_in_bounds")
+                    value = got if value is None else jnp.where(chosen >= plane * 8, got, value)
+                base = first * rows + slot * (fields + 1) + f
+                out_ref[pl.ds(base, 8, stride=rows), :] = value
+
+
+def route(records, selection, groups, capacity, rows, fields, out_ref):
+    coarse_depth = out_ref.shape[1]
     total = records.shape[0] // fields
     wide = jnp.concatenate(
         [records[f * total:(f + 1) * total] for f in range(fields)], axis=1
@@ -486,8 +537,8 @@
     total = owner_ref.shape[1]
     selections = one_hot_slots(owner_ref[...], groups, capacity)
     route(
-        jnp.concatenate(blocks, axis=0), jnp.concatenate(selections, axis=0),
-        groups, capacity, rows, fields, out_ref,
+        pool_z(jnp.concatenate(blocks, axis=0), out_ref.shape[1]),
+        jnp.concatenate(selections, axis=0), groups, capacity, rows, fields, out_ref,
     )
     record_ids = lax.broadcasted_iota(jnp.int32, (1, total), 1)
     codes = (column_ref[...] + 1).astype(jnp.float32)
@@ -570,16 +621,19 @@
         shapes = [
             current.shape,
             (2, 3 * fields, 2, half_across, cells_depth),
-            (fields, half_across, cells_depth),
-            (cells_along // 2 - 1, fields, half_across, cells_depth),
-            (capacity * group_count, total),
+            (fields, half_across, coarse_depth),
+            (cells_along // 2 - 1, fields, half_across, coarse_depth),
+            (capacity * group_count, coarse_depth),
             (capacity * group_count, coarse_depth),
             owned_state.shape,
             owned_term.shape,
         ]
         early, carry, face, sums, selection, codes, owned_state, owned_term = pl.pallas_call(
             functools.partial(early_kernel, group_count, capacity),
-            out_shape=[pltpu.VMEM(shape, jnp.float32) for shape in shapes],
+            out_shape=[
+                pltpu.VMEM(shape, jnp.int32 if index == 4 else jnp.float32)
+                for index, shape in enumerate(shapes)
+            ],
             in_specs=[hbm] * 6,
             out_specs=[vmem] * len(shapes),
             scratch_shapes=[

time: 20.5 us -> 20.2 us (0.985)
  Pallas kernels: 3.75 us -> 3.43 us
    pallas_call x1, Pallas kernels: 0.68 us -> 0.41 us  [on_device(): pl.pallas_call(functools.partial(late_kernel, group_count, capacity, rows...]
where the time goes in v4:
time: 20.2 us; the launch traced here: 20 us
  blocking collectives  15.4 us (76%)
  Pallas kernels  3.43 us (17%)
  between operations  0.66 us (3%)
  starting transfers between devices  0.56 us (3%)
    all_to_all x1, blocking collectives, on_device(): lax.all_to_all(outgoing.reshape(group_count, rows // inner_rows, inner_ro...  15.4 us
    pallas_call x1, Pallas kernels, on_device(): pl.pallas_call(functools.partial(early_kernel, group_count, capacity), ou...  2.14 us
    pallas_call x1, Pallas kernels, on_device(): pl.pallas_call(functools.partial(owner_kernel, group_count, capacity, row...  0.88 us
    ppermute x1, starting transfers between devices, on_device(): other = lax.ppermute(current, 'box', [(0, 1), (1, 0)])  0.56 us
    pallas_call x1, Pallas kernels, on_device(): pl.pallas_call(functools.partial(late_kernel, group_count, capacity, rows...  0.41 us
  transfers between devices with their start and end apart: 1, of which 0 were waited for; matrix products, arithmetic and copies ran while one was open for 0% of the time, Pallas kernels for 11%

profile of v4, /device:TPU:0, one launch (start us, length us, event | category | flops | bytes accessed | tf_op | source)
XLA Modules:
  0.0 20.0 jit_solution(6746646397418764453)
XLA Ops:
  0.6 0.6 %collective-permute-start = (f32[5,4,16,256]{3,2,1,0:T(8,128)}, f32[5,4,16,256]{3,2,1,0:T(8,128)S(1)}, u32[]{:S(2)}, u32[]{:S(2)}) collective-permute-start(f32[5,4,16,256]{3,2,1,0:T(8,128)} %bitcast.17), channel_id=1, source_target_pairs={{0,1},{1,0},{2,3},{3,2},{4,5},{5,4},{6,7},{7,6},{8,9},{9,8},{10,11... | collective-permute-start | bytes 983048 | tf_op jit(solution)/shard_map/ppermute | solution.py:619
  1.2 2.1 %early.1 = (f32[5,4,16,256]{3,2,1,0:T(8,128)S(1)}, f32[2,15,2,8,256]{4,3,2,1,0:T(8,128)S(1)}, f32[5,8,128]{2,1,0:T(8,128)S(1)}, f32[1,5,8,128]{3,2,1,0:T(8,128)S...) custom-call(f32[1,5,4,16,256]{4,3,2,1,0:T(8,128)} %fine_ref.1, ...), custom_call_target="tpu_custom_call" | custom-call | flops 16384000 | bytes 655360 | tf_op jit(solution)/shard_map/early/pallas_call | solution.py:631
  3.3 0.0 collective-permute-done.other_ref
  3.3 0.4 %late.1 = (f32[5,4,16,256]{3,2,1,0:T(8,128)S(1)}, f32[192,128]{1,0:T(8,128)S(1)}) custom-call(f32[2,15,2,8,256]{4,3,2,1,0:T(8,128)S(1)} %get-tuple-element.14.carry_ref, f32[5,4,16,256]{3,2,1,0:T(8,128)S(1)} %collective-permute-done.other_ref, f32[5,8,128]{2,1,0:T(8,128)S(1)} %get-tuple-element.15.face_ref, ...), custom_call_target="tpu_custom_call", output_to_operand_aliasing={{0}: (6, {})} | custom-call | tf_op jit(solution)/shard_map/late/pallas_call | solution.py:656
  3.8 15.4 %all_to_all.5 = f32[16,3,4,128]{3,2,1,0:T(4,128)S(1)} all-to-all(f32[16,3,4,128]{3,2,1,0:T(4,128)S(1)} %bitcast.16), channel_id=1, replica_groups=mesh['grp'=16,'box'=2] {'grp'}, dimensions={0} | all-to-all | bytes 196608 | tf_op jit(solution)/shard_map/all_to_all | solution.py:685
  19.1 0.9 %owner.1 = (f32[5,24,128]{2,1,0:T(8,128)}, f32[5,4,16,256]{3,2,1,0:T(8,128)}) custom-call(f32[192,128]{1,0:T(8,128)S(1)} %bitcast.15, f32[5,24,128]{2,1,0:T(8,128)S(1)} %get-tuple-element.21.state_ref, f32[5,24,128]{2,1,0:T(8,128)S(1)} %get-tuple-element.22.term_ref, f32[5,4,16,256]{3,2,1,0:T(8,128)S(1)} %get-tuple-element.23.new_ref), custom_call_target="tpu_custom_call" | custom-call | tf_op jit(solution)/shard_map/owner/pallas_call | solution.py:689
Async XLA Ops:
  0.6 2.7 %collective-permute-start = (f32[5,4,16,256]{3,2,1,0:T(8,128)}, f32[5,4,16,256]{3,2,1,0:T(8,128)S(1)}, u32[]{:S(2)}, u32[]{:S(2)}) collective-permute-start(f32[5,4,16,256]{3,2,1,0:T(8,128)} %bitcast.17), channel_id=1, source_target_pairs={{0,1},{1,0},{2,3},{3,2},{4,5},{5,4},{6,7},{7,6},{8,9},{9,8},{10,11... | collective-permute-start | bytes 983048 | tf_op jit(solution)/shard_map/ppermute | solution.py:619

commit v5 on v4

--- a/solution.py
+++ b/solution.py
@@ -558,36 +558,41 @@
     write_fine = pltpu.make_async_copy(new_ref, final_ref, copy_sems.at[0])
     write_fine.start()
     fields, total, coarse_depth = state_ref.shape
-    codes, values = [], []
-    for slot in range(capacity):
-        base = slot * (fields + 1)
-        code = in_ref[pl.ds(base + fields, groups, stride=rows), :]
-        codes.append(code)
-        values.append(
-            jnp.concatenate(
-                [
-                    jnp.where(code != 0.0, in_ref[pl.ds(base + f, groups, stride=rows), :], 0.0)
-                    for f in range(fields)
-                ],
-                axis=1,
-            )
-        )
-    codes = jnp.concatenate(codes, axis=0)
-    values = jnp.concatenate(values, axis=0)
+    codes = jnp.concatenate(
+        [
+            in_ref[pl.ds(slot * (fields + 1) + fields, groups, stride=rows), :]
+            for slot in range(capacity)
+        ],
+        axis=0,
+    )
     count = codes.shape[0]
     across = jnp.transpose(codes)[:total]
     column = (lax.broadcasted_iota(jnp.int32, (total, count), 0) + 1).astype(jnp.float32)
-    hot = jnp.where(jnp.abs(across) == column, 1.0, 0.0)
-    kind = jnp.where(codes > 0.0, 1.0, jnp.where(codes < 0.0, -1.0, 0.0))
-    flag = jnp.dot(
-        hot.astype(jnp.bfloat16), kind.astype(jnp.bfloat16), preferred_element_type=jnp.float32
-    )
-    got = split_dot(hot, values, False)
-    for f in range(fields):
-        value = got[:, f * coarse_depth:(f + 1) * coarse_depth]
-        state = state_ref[f]
-        refluxed = state + (value - term_ref[f])
-        out_ref[f] = jnp.where(flag > 0.0, value, jnp.where(flag < 0.0, refluxed, state))
+    hit = jnp.abs(across) == column
+    place = lax.broadcasted_iota(jnp.int32, (total, count), 1).astype(jnp.float32)
+    source = jnp.sum(jnp.where(hit, place, 0.0), axis=1, keepdims=True)
+    kind = jnp.sum(jnp.where(hit, across, 0.0), axis=1, keepdims=True)
+    source = jnp.broadcast_to(source, (total, coarse_depth)).astype(jnp.int32)
+    kind = jnp.broadcast_to(kind, (total, coarse_depth))
+    for first in range(0, total, 8):
+        part = slice(first, first + 8)
+        chosen, sign = source[part], kind[part]
+        row = chosen & 7
+        for f in range(fields):
+            value = None
+            for at in range(0, count, 8):
+                slot, group = at // groups, at % groups
+                base = group * rows + slot * (fields + 1) + f
+                got = jnp.take_along_axis(
+                    in_ref[pl.ds(base, 8, stride=rows), :], row,
+                    axis=0, mode="promise_in_bounds",
+                )
+                value = got if value is None else jnp.where(chosen >= at, got, value)
+            state = state_ref[f, part]
+            refluxed = state + (value - term_ref[f, part])
+            out_ref[f, part] = jnp.where(
+                sign > 0.0, value, jnp.where(sign < 0.0, refluxed, state)
+            )
     write_coarse = pltpu.make_async_copy(out_ref, coarse_ref, copy_sems.at[1])
     write_coarse.start()
     write_fine.wait()

time: 20.2 us -> 20.2 us (level)
  no operation moved by 1% of the time
where the time goes in v5:
time: 20.2 us; the launch traced here: 20 us
  blocking collectives  15.4 us (76%)
  Pallas kernels  3.37 us (17%)
  between operations  0.66 us (3%)
  starting transfers between devices  0.56 us (3%)
    all_to_all x1, blocking collectives, on_device(): lax.all_to_all(outgoing.reshape(group_count, rows // inner_rows, inner_ro...  15.4 us
    pallas_call x1, Pallas kernels, on_device(): pl.pallas_call(functools.partial(early_kernel, group_count, capacity), ou...  2.14 us
    pallas_call x1, Pallas kernels, on_device(): pl.pallas_call(functools.partial(owner_kernel, group_count, capacity, row...  0.82 us
    ppermute x1, starting transfers between devices, on_device(): other = lax.ppermute(current, 'box', [(0, 1), (1, 0)])  0.56 us
    pallas_call x1, Pallas kernels, on_device(): pl.pallas_call(functools.partial(late_kernel, group_count, capacity, rows...  0.41 us
  transfers between devices with their start and end apart: 1, of which 0 were waited for; matrix products, arithmetic and copies ran while one was open for 0% of the time, Pallas kernels for 11%

profile of v5, /device:TPU:0, one launch (start us, length us, event | category | flops | bytes accessed | tf_op | source)
XLA Modules:
  0.0 20.0 jit_solution(2191174193065792117)
XLA Ops:
  0.6 0.6 %collective-permute-start = (f32[5,4,16,256]{3,2,1,0:T(8,128)}, f32[5,4,16,256]{3,2,1,0:T(8,128)S(1)}, u32[]{:S(2)}, u32[]{:S(2)}) collective-permute-start(f32[5,4,16,256]{3,2,1,0:T(8,128)} %bitcast.17), channel_id=1, source_target_pairs={{0,1},{1,0},{2,3},{3,2},{4,5},{5,4},{6,7},{7,6},{8,9},{9,8},{10,11... | collective-permute-start | bytes 983048 | tf_op jit(solution)/shard_map/ppermute | solution.py:624
  1.2 2.1 %early.1 = (f32[5,4,16,256]{3,2,1,0:T(8,128)S(1)}, f32[2,15,2,8,256]{4,3,2,1,0:T(8,128)S(1)}, f32[5,8,128]{2,1,0:T(8,128)S(1)}, f32[1,5,8,128]{3,2,1,0:T(8,128)S...) custom-call(f32[1,5,4,16,256]{4,3,2,1,0:T(8,128)} %fine_ref.1, ...), custom_call_target="tpu_custom_call" | custom-call | flops 16384000 | bytes 655360 | tf_op jit(solution)/shard_map/early/pallas_call | solution.py:636
  3.3 0.0 collective-permute-done.other_ref
  3.3 0.4 %late.1 = (f32[5,4,16,256]{3,2,1,0:T(8,128)S(1)}, f32[192,128]{1,0:T(8,128)S(1)}) custom-call(f32[2,15,2,8,256]{4,3,2,1,0:T(8,128)S(1)} %get-tuple-element.14.carry_ref, f32[5,4,16,256]{3,2,1,0:T(8,128)S(1)} %collective-permute-done.other_ref, f32[5,8,128]{2,1,0:T(8,128)S(1)} %get-tuple-element.15.face_ref, ...), custom_call_target="tpu_custom_call", output_to_operand_aliasing={{0}: (6, {})} | custom-call | tf_op jit(solution)/shard_map/late/pallas_call | solution.py:661
  3.8 15.4 %all_to_all.5 = f32[16,3,4,128]{3,2,1,0:T(4,128)S(1)} all-to-all(f32[16,3,4,128]{3,2,1,0:T(4,128)S(1)} %bitcast.16), channel_id=1, replica_groups=mesh['grp'=16,'box'=2] {'grp'}, dimensions={0} | all-to-all | bytes 196608 | tf_op jit(solution)/shard_map/all_to_all | solution.py:690
  19.1 0.8 %owner.1 = (f32[5,24,128]{2,1,0:T(8,128)}, f32[5,4,16,256]{3,2,1,0:T(8,128)}) custom-call(f32[192,128]{1,0:T(8,128)S(1)} %bitcast.15, f32[5,24,128]{2,1,0:T(8,128)S(1)} %get-tuple-element.21.state_ref, f32[5,24,128]{2,1,0:T(8,128)S(1)} %get-tuple-element.22.term_ref, f32[5,4,16,256]{3,2,1,0:T(8,128)S(1)} %get-tuple-element.23.new_ref), custom_call_target="tpu_custom_call" | custom-call | tf_op jit(solution)/shard_map/owner/pallas_call | solution.py:694
Async XLA Ops:
  0.6 2.7 %collective-permute-start = (f32[5,4,16,256]{3,2,1,0:T(8,128)}, f32[5,4,16,256]{3,2,1,0:T(8,128)S(1)}, u32[]{:S(2)}, u32[]{:S(2)}) collective-permute-start(f32[5,4,16,256]{3,2,1,0:T(8,128)} %bitcast.17), channel_id=1, source_target_pairs={{0,1},{1,0},{2,3},{3,2},{4,5},{5,4},{6,7},{7,6},{8,9},{9,8},{10,11... | collective-permute-start | bytes 983048 | tf_op jit(solution)/shard_map/ppermute | solution.py:624

commit v6 on v5

--- a/solution.py
+++ b/solution.py
@@ -194,6 +194,17 @@
     def finished(self, high_face):
         half = 0.5 * time_step
         return [both(lambda p, h: p - half * h, p, h) for p, h in zip(self.partial, high_face)]
+
+
+def joined_codes(selections, codes, lanes):
+    groups, share = selections[0].shape[0], lanes // len(selections)
+    at = lax.broadcasted_iota(jnp.int32, (groups, lanes), 1)
+    joined = None
+    for slot, selection in enumerate(selections):
+        code = jnp.sum(selection * codes, axis=1, keepdims=True)
+        code = jnp.broadcast_to(code, (groups, lanes))
+        joined = code if joined is None else jnp.where(at >= slot * share, code, joined)
+    return joined
 
 
 def early_kernel(
@@ -310,8 +321,7 @@
         ids = record_ids.astype(jnp.float32)
         record = jnp.sum(selections[slot] * ids, axis=1, keepdims=True)
         select_ref[rows] = jnp.broadcast_to(record, (groups, code_ref.shape[1])).astype(jnp.int32)
-        code = jnp.sum(selections[slot] * codes, axis=1, keepdims=True)
-        code_ref[rows] = jnp.broadcast_to(code, (groups, code_ref.shape[1]))
+    code_ref[...] = joined_codes(selections, codes, code_ref.shape[1])
 
 
 def late_kernel(
@@ -374,10 +384,7 @@
         record_ids = lax.broadcasted_iota(jnp.int32, (capacity * groups, total), 1)
         chosen = jnp.where(select_ref[:, :1] == record_ids, 1.0, 0.0)
         route(joined, chosen, groups, capacity, rows, fields, out_ref)
-    for slot in range(capacity):
-        out_ref[pl.ds(slot * (fields + 1) + fields, groups, stride=rows), :] = code_ref[
-            slot * groups:(slot + 1) * groups
-        ]
+    out_ref[pl.ds(capacity * fields, groups, stride=rows), :] = code_ref[...]
 
 
 def pool_z(stacked, coarse_depth):
@@ -419,7 +426,7 @@
                 for plane, record in enumerate(records[f]):
                     got = jnp.take_along_axis(record, row, axis=0, mode="promise_in_bounds")
                     value = got if value is None else jnp.where(chosen >= plane * 8, got, value)
-                base = first * rows + slot * (fields + 1) + f
+                base = first * rows + slot * fields + f
                 out_ref[pl.ds(base, 8, stride=rows), :] = value
 
 
@@ -432,7 +439,7 @@
     chosen = split_dot(selection, wide, False)
     for slot in range(capacity):
         for f in range(fields):
-            out_ref[pl.ds(slot * (fields + 1) + f, groups, stride=rows), :] = chosen[
+            out_ref[pl.ds(slot * fields + f, groups, stride=rows), :] = chosen[
                 slot * groups:(slot + 1) * groups, f * coarse_depth:(f + 1) * coarse_depth
             ]
 
@@ -544,11 +551,9 @@
     codes = (column_ref[...] + 1).astype(jnp.float32)
     face_code = jnp.where(at_low | at_high, -codes, 0.0)
     codes = jnp.where(record_ids < planes * half_across, codes, face_code)
-    for slot in range(capacity):
-        code = jnp.sum(selections[slot] * codes, axis=1, keepdims=True)
-        out_ref[pl.ds(slot * (fields + 1) + fields, groups, stride=rows), :] = jnp.broadcast_to(
-            code, (groups, out_ref.shape[1])
-        )
+    out_ref[pl.ds(capacity * fields, groups, stride=rows), :] = joined_codes(
+        selections, codes, out_ref.shape[1]
+    )
 
 
 def owner_kernel(
@@ -558,20 +563,18 @@
     write_fine = pltpu.make_async_copy(new_ref, final_ref, copy_sems.at[0])
     write_fine.start()
     fields, total, coarse_depth = state_ref.shape
-    codes = jnp.concatenate(
-        [
-            in_ref[pl.ds(slot * (fields + 1) + fields, groups, stride=rows), :]
-            for slot in range(capacity)
-        ],
-        axis=0,
-    )
-    count = codes.shape[0]
-    across = jnp.transpose(codes)[:total]
-    column = (lax.broadcasted_iota(jnp.int32, (total, count), 0) + 1).astype(jnp.float32)
-    hit = jnp.abs(across) == column
-    place = lax.broadcasted_iota(jnp.int32, (total, count), 1).astype(jnp.float32)
-    source = jnp.sum(jnp.where(hit, place, 0.0), axis=1, keepdims=True)
-    kind = jnp.sum(jnp.where(hit, across, 0.0), axis=1, keepdims=True)
+    count, share = capacity * groups, coarse_depth // capacity
+    lanes = jnp.transpose(in_ref[pl.ds(capacity * fields, groups, stride=rows), :])
+    column = (lax.broadcasted_iota(jnp.int32, (total, groups), 0) + 1).astype(jnp.float32)
+    place = lax.broadcasted_iota(jnp.int32, (total, groups), 1).astype(jnp.float32)
+    places = kinds = jnp.zeros((total, groups), jnp.float32)
+    for slot in range(capacity):
+        across = lanes[slot * share:slot * share + total]
+        hit = jnp.abs(across) == column
+        places = jnp.where(hit, place + float(slot * groups), places)
+        kinds = jnp.where(hit, across, kinds)
+    source = jnp.sum(places, axis=1, keepdims=True)
+    kind = jnp.sum(kinds, axis=1, keepdims=True)
     source = jnp.broadcast_to(source, (total, coarse_depth)).astype(jnp.int32)
     kind = jnp.broadcast_to(kind, (total, coarse_depth))
     for first in range(0, total, 8):
@@ -582,7 +585,7 @@
             value = None
             for at in range(0, count, 8):
                 slot, group = at // groups, at % groups
-                base = group * rows + slot * (fields + 1) + f
+                base = group * rows + slot * fields + f
                 got = jnp.take_along_axis(
                     in_ref[pl.ds(base, 8, stride=rows), :], row,
                     axis=0, mode="promise_in_bounds",
@@ -606,7 +609,7 @@
     fields, cells_along, cells_across, cells_depth = current.shape
     total = dest_grp.shape[-1]
     capacity = (total + group_count - 1) // group_count
-    rows = capacity * (fields + 1)
+    rows = capacity * fields + 1
     inner_rows = math.gcd(rows, 8)
     coarse_depth = cells_depth // 2
     owned_state = coarse_state[0, 0].transpose(1, 0, 2)
@@ -629,7 +632,7 @@
             (fields, half_across, coarse_depth),
             (cells_along // 2 - 1, fields, half_across, coarse_depth),
             (capacity * group_count, coarse_depth),
-            (capacity * group_count, coarse_depth),
+            (group_count, coarse_depth),
             owned_state.shape,
             owned_term.shape,
         ]

time: 20.2 us -> 20.1 us (level)
  no operation moved by 1% of the time
where the time goes in v6:
time: 20.1 us; the launch traced here: 19.9 us
  blocking collectives  15.3 us (76%)
  Pallas kernels  3.39 us (17%)
  between operations  0.66 us (3%)
  starting transfers between devices  0.56 us (3%)
    all_to_all x1, blocking collectives, on_device(): lax.all_to_all(outgoing.reshape(group_count, rows // inner_rows, inner_ro...  15.3 us
    pallas_call x1, Pallas kernels, on_device(): pl.pallas_call(functools.partial(early_kernel, group_count, capacity), ou...  2.14 us
    pallas_call x1, Pallas kernels, on_device(): pl.pallas_call(functools.partial(owner_kernel, group_count, capacity, row...  0.84 us
    ppermute x1, starting transfers between devices, on_device(): other = lax.ppermute(current, 'box', [(0, 1), (1, 0)])  0.56 us
    pallas_call x1, Pallas kernels, on_device(): pl.pallas_call(functools.partial(late_kernel, group_count, capacity, rows...  0.41 us
  transfers between devices with their start and end apart: 1, of which 0 were waited for; matrix products, arithmetic and copies ran while one was open for 0% of the time, Pallas kernels for 11%

profile of v6, /device:TPU:0, one launch (start us, length us, event | category | flops | bytes accessed | tf_op | source)
XLA Modules:
  0.0 19.9 jit_solution(15988308171331127857)
XLA Ops:
  0.6 0.6 %collective-permute-start = (f32[5,4,16,256]{3,2,1,0:T(8,128)}, f32[5,4,16,256]{3,2,1,0:T(8,128)S(1)}, u32[]{:S(2)}, u32[]{:S(2)}) collective-permute-start(f32[5,4,16,256]{3,2,1,0:T(8,128)} %bitcast.17), channel_id=1, source_target_pairs={{0,1},{1,0},{2,3},{3,2},{4,5},{5,4},{6,7},{7,6},{8,9},{9,8},{10,11... | collective-permute-start | bytes 983048 | tf_op jit(solution)/shard_map/ppermute | solution.py:627
  1.2 2.1 %early.1 = (f32[5,4,16,256]{3,2,1,0:T(8,128)S(1)}, f32[2,15,2,8,256]{4,3,2,1,0:T(8,128)S(1)}, f32[5,8,128]{2,1,0:T(8,128)S(1)}, f32[1,5,8,128]{3,2,1,0:T(8,128)S...) custom-call(f32[1,5,4,16,256]{4,3,2,1,0:T(8,128)} %fine_ref.1, ...), custom_call_target="tpu_custom_call" | custom-call | flops 16384000 | bytes 655360 | tf_op jit(solution)/shard_map/early/pallas_call | solution.py:639
  3.3 0.0 collective-permute-done.other_ref
  3.3 0.4 %late.1 = (f32[5,4,16,256]{3,2,1,0:T(8,128)S(1)}, f32[176,128]{1,0:T(8,128)S(1)}) custom-call(f32[2,15,2,8,256]{4,3,2,1,0:T(8,128)S(1)} %get-tuple-element.14.carry_ref, f32[5,4,16,256]{3,2,1,0:T(8,128)S(1)} %collective-permute-done.other_ref, f32[5,8,128]{2,1,0:T(8,128)S(1)} %get-tuple-element.15.face_ref, ...), custom_call_target="tpu_custom_call", output_to_operand_aliasing={{0}: (6, {})} | custom-call | tf_op jit(solution)/shard_map/late/pallas_call | solution.py:664
  3.8 15.3 %all_to_all.5 = f32[16,11,1,128]{3,2,1,0:T(1,128)S(1)} all-to-all(f32[16,11,1,128]{3,2,1,0:T(1,128)S(1)} %bitcast.16), channel_id=1, replica_groups=mesh['grp'=16,'box'=2] {'grp'}, dimensions={0} | all-to-all | bytes 180224 | tf_op jit(solution)/shard_map/all_to_all | solution.py:693
  19.1 0.8 %owner.1 = (f32[5,24,128]{2,1,0:T(8,128)}, f32[5,4,16,256]{3,2,1,0:T(8,128)}) custom-call(f32[176,128]{1,0:T(8,128)S(1)} %bitcast.15, f32[5,24,128]{2,1,0:T(8,128)S(1)} %get-tuple-element.21.state_ref, f32[5,24,128]{2,1,0:T(8,128)S(1)} %get-tuple-element.22.term_ref, f32[5,4,16,256]{3,2,1,0:T(8,128)S(1)} %get-tuple-element.23.new_ref), custom_call_target="tpu_custom_call" | custom-call | tf_op jit(solution)/shard_map/owner/pallas_call | solution.py:697
Async XLA Ops:
  0.6 2.7 %collective-permute-start = (f32[5,4,16,256]{3,2,1,0:T(8,128)}, f32[5,4,16,256]{3,2,1,0:T(8,128)S(1)}, u32[]{:S(2)}, u32[]{:S(2)}) collective-permute-start(f32[5,4,16,256]{3,2,1,0:T(8,128)} %bitcast.17), channel_id=1, source_target_pairs={{0,1},{1,0},{2,3},{3,2},{4,5},{5,4},{6,7},{7,6},{8,9},{9,8},{10,11... | collective-permute-start | bytes 983048 | tf_op jit(solution)/shard_map/ppermute | solution.py:627
